TPU v7x, 128 devices: a whole 4x4x4 slice. The times are simulated.
128 devices in a mesh: batch: 4 (over z), seq: 16 (over y, x_lo, core), head: 2 (over x_hi).
Axes of the slice: x: 4 (x_hi: 2, x_lo: 2; x = x_hi * 2 + x_lo), y: 4, z: 4, core: 2. Of those that a mesh axis runs over, the one named last changes fastest.
Arguments:
- image_hidden: bfloat16 [8, 4096, 3072], P('batch', 'seq', 'head'), parts along dimension 0, may hold values from -6 to 6
- modulation: float32 [8, 3, 3072], P('batch'), parts along dimension 0, may hold values from -4 to 4
- qkv_weight: bfloat16 [3072, 3, 1536], P(None, None, 'head'), may hold values from -0.109375 to 0.109375
- out_weight: bfloat16 [1536, 3072], P('head'), may hold values from -0.15625 to 0.15625
- q_gain: float32 [128], replicated, may hold values from 1.2 to 2.5
- k_gain: float32 [128], replicated, may hold values from 1.2 to 2.5
- text_keys: bfloat16 [8, 512, 1536], P('batch', 'seq', 'head'), parts along dimension 0, may hold values from -10 to 10
- text_values: bfloat16 [8, 512, 1536], P('batch', 'seq', 'head'), parts along dimension 0, may hold values from -6 to 6
- stale_keys: bfloat16 [8, 4096, 1536], P('batch', 'seq', 'head'), parts along dimension 0, may hold values from -64 to 64
- stale_values: bfloat16 [8, 4096, 1536], P('batch', 'seq', 'head'), parts along dimension 0, may hold values from -6 to 6
- cached_residual: bfloat16 [8, 4096, 3072], P('batch', 'seq', 'head'), parts along dimension 0, may hold values from -6 to 6
- patch_of: int32 [64], P('batch'), parts along dimension 0, may hold values from 0 to 15, each once
- refresh: int32 [64], P('batch'), parts along dimension 0, may hold values from 0 to 1, as said below
- text_len: int32 [8], P('batch'), parts along dimension 0, may hold values from 64 to 512
Outputs:
- image_out: bfloat16 [8, 4096, 3072], P('batch', 'seq', 'head'), parts along dimension 0
There are 4 independent parts, one for each index of `batch`. A program takes and returns all parts, laid end to end along the dimension named above; an argument that names none is the same for every part. Nothing has to cross between parts.
Inputs may be any that keep to these rules, and one draw needn't show every extreme that they name: `patch_of`: A permutation: every image band sits on exactly one index of seq. `refresh`: exactly 4 entries are 1, the rest 0.
All inputs are finite; a program needn't handle non-finite values.
Results may differ from a plain program's by a relative error of at most 0.012.
The roundings to bfloat16 on the way count: a program that leaves them out, or rounds other values in their place, can miss the bound.
Values may be sent and summed in bfloat16 or wider, within the bound.
No kernel may reach another device: no remote copies, remote signals or barrier semaphores. Data moves between devices by JAX's collectives and lax.ppermute only.
A program may use at most 192 MiB of HBM per device.

v0:
```python
import jax
import jax.numpy as jnp
from jax import lax
from jax.experimental import pallas as pl
from jax.experimental.pallas import tpu as pltpu
from jax.sharding import PartitionSpec as P


GRID_W = 64
EPS = 1e-06
LOG2E = 1.4426950408889634
F32 = jnp.float32
BF16 = jnp.bfloat16
NEG = -1e30
VMEM = 56 * 1024 * 1024
SLOTS = 8


def rotary_tables(raster, head_dim, grid_width):
    half_dim = head_dim // 2
    first_pairs = head_dim // 16
    axis_pairs = (half_dim - first_pairs) // 2
    pair_index = jnp.arange(half_dim, dtype=jnp.int32)
    pair_local = jnp.where(
        pair_index < first_pairs + axis_pairs,
        pair_index - first_pairs,
        pair_index - first_pairs - axis_pairs,
    )
    exponent = -pair_local.astype(F32) / float(axis_pairs)
    frequency = jnp.where(pair_index < first_pairs, F32(0.0), jnp.power(F32(10000.0), exponent))
    row_pos = (raster // grid_width).astype(F32)
    col_pos = (raster % grid_width).astype(F32)
    position = jnp.where(
        pair_index[None, :] < first_pairs + axis_pairs, row_pos[:, None], col_pos[:, None]
    )
    angles = position * frequency[None, :]
    cosine = jnp.cos(angles)
    sine = jnp.sin(angles)
    return (jnp.concatenate([cosine, cosine], axis=-1), jnp.concatenate([-sine, sine], axis=-1))


def qkv_body(
    info, own, oth, mod_own, mod_oth, w_own, w_oth, gains, cos, sin, stale_k, stale_v, send, fresh, mod_s, wide_s
):
    n = pl.program_id(0)
    prompts, rows, part = own.shape
    width = 2 * part
    tile = 16

    @pl.when(n == 0)
    def _():
        for p in range(prompts):
            for k in range(2):
                for m, mod in enumerate((mod_own, mod_oth)):
                    row = mod[k, p : p + 1, :] + float(k)
                    wide_s[k, :, m * part : (m + 1) * part] = jnp.broadcast_to(row, (8, part))

            def norm(i, c):
                at = pl.multiple_of(i * tile, tile)
                a = own[p, pl.ds(at, tile), :].astype(F32)
                b = oth[p, pl.ds(at, tile), :].astype(F32)
                mean = (jnp.sum(a, -1, keepdims=True) + jnp.sum(b, -1, keepdims=True)) / width
                a, b = a - mean, b - mean
                var = (jnp.sum(a * a, -1, keepdims=True) + jnp.sum(b * b, -1, keepdims=True)) / width
                inv = lax.rsqrt(var + EPS)
                a = moved(a * inv, 0)
                b = moved(b * inv, part)
                to = pl.multiple_of(p * rows + i * tile, tile)
                mod_s[pl.ds(to, tile), 0:part] = a.astype(BF16)
                mod_s[pl.ds(to, tile), part:width] = b.astype(BF16)
                return c

            def moved(x, at):
                shift, scale = (wide_s[k, :, at : at + part] for k in range(2))
                parts = [x[r : r + 8] * scale + shift for r in range(0, tile, 8)]
                return jnp.concatenate(parts, 0)

            lax.fori_loop(0, rows // tile, norm, 0, unroll=4)

    heads = w_own.shape[2] // 128
    per = 2
    flag = info[1]

    def products():
        for j in range(0, heads, per):
            cols = slice(j * 128, (j + per) * 128)
            acc = jnp.dot(mod_s[:, 0:part], w_own[0, :, cols], preferred_element_type=F32)
            acc = acc + jnp.dot(mod_s[:, part:width], w_oth[0, :, cols], preferred_element_type=F32)
            for p in range(prompts):
                for e in range(per):
                    yield p, j + e, acc[p * rows : (p + 1) * rows, e * 128 : (e + 1) * 128]

    def turned(x, gain):
        x = x * lax.rsqrt(jnp.mean(x * x, axis=-1, keepdims=True) + EPS) * gain
        return x * cos[...] + pltpu.roll(x, 64, 1) * sin[...]

    @pl.when(n == 0)
    def _():
        for p, j, x in products():
            send[p, j, 0] = turned(x, gains[0:1, :]).astype(BF16)

    @pl.when(n == 1)
    def _():
        for p, j, x in products():
            new = turned(x, gains[1:2, :]).astype(BF16)
            fresh[p, j, 0] = new
            send[p, j, 0] = jnp.where(flag == 1, new, stale_k[p, :, j * 128 : (j + 1) * 128])

    @pl.when(n == 2)
    def _():
        for p, j, x in products():
            new = x.astype(BF16)
            used = jnp.where(flag == 1, new, stale_v[p, :, j * 128 : (j + 1) * 128])
            for r in range(0, rows, 128):
                fresh[p, j, 0, r : r + 128, :] = jnp.transpose(new[r : r + 128, :])
                send[p, j, 0, r : r + 128, :] = jnp.transpose(used[r : r + 128, :])


def qkv(c, info, own, oth, modulation, w, gains, cos, sin, stale_k, stale_v):
    prompts, rows, part = oth.shape
    channels = stale_k.shape[2]
    heads = channels // 128
    whole = lambda *shape: pl.BlockSpec(shape, lambda n, s: (0,) * len(shape))
    half = lambda *shape: pl.BlockSpec(shape, lambda n, s: (0, c, 0))
    return pl.pallas_call(
        qkv_body,
        grid_spec=pltpu.PrefetchScalarGridSpec(
            num_scalar_prefetch=1,
            grid=(3,),
            in_specs=[
                half(prompts, rows, part),
                whole(prompts, rows, part),
                pl.BlockSpec((3, prompts, part), lambda n, s: (0, 0, s[0])),
                pl.BlockSpec((3, prompts, part), lambda n, s: (0, 0, 1 - s[0])),
                pl.BlockSpec((1, part, channels), lambda n, s: (n, s[0], 0)),
                pl.BlockSpec((1, part, channels), lambda n, s: (n, 1 - s[0], 0)),
                whole(2, 128),
                pl.BlockSpec((rows, 128), lambda n, s: (c, 0)),
                pl.BlockSpec((rows, 128), lambda n, s: (c, 0)),
                half(prompts, rows, channels),
                half(prompts, rows, channels),
            ],
            out_specs=[
                pl.BlockSpec((prompts, SLOTS, 1, rows, 128), lambda n, s: (0, 0, n, 0, 0)),
                pl.BlockSpec(
                    (prompts, heads, 1, rows, 128), lambda n, s: (0, 0, jnp.maximum(n - 1, 0), 0, 0)
                ),
            ],
            scratch_shapes=[
                pltpu.VMEM((prompts * rows, 2 * part), BF16),
                pltpu.VMEM((2, 8, 2 * part), F32),
            ],
        ),
        out_shape=[
            jax.ShapeDtypeStruct((prompts, SLOTS, 3, rows, 128), BF16),
            jax.ShapeDtypeStruct((prompts, heads, 2, rows, 128), BF16),
        ],
        compiler_params=pltpu.CompilerParams(
            dimension_semantics=("arbitrary",), vmem_limit_bytes=VMEM
        ),
        cost_estimate=pl.CostEstimate(
            flops=2 * prompts * rows * 2 * part * 3 * channels, bytes_accessed=20_000_000, transcendentals=0
        ),
        name="qkv",
    )(info, own, oth, modulation, modulation, w, w, gains, cos, sin, stale_k, stale_v)


CONTRACT = (((1,), (1,)), ((), ()))


def log_sum_rows(lse):
    lse = jnp.broadcast_to(lse, (16, lse.shape[1]))
    first = lse.astype(BF16).astype(F32)
    second = (lse - first).astype(BF16).astype(F32)
    third = lse - first - second
    at = lax.broadcasted_iota(jnp.int32, lse.shape, 0)
    return jnp.where(at == 0, first, jnp.where(at == 1, second, third)).astype(BF16)


def diag_body(*refs):
    halves = len(refs) // 2
    send, fresh, out = refs[:halves], refs[halves : 2 * halves], refs[-1]
    c = 128**-0.5 * LOG2E
    for e in range(out.shape[1]):
        q = jnp.concatenate([r[0, e, 0] for r in send], 0)
        k = jnp.concatenate([r[0, e, 0] for r in fresh], 0)
        v = jnp.concatenate([r[0, e, 1] for r in fresh], 1)
        s = lax.dot_general(k, q, CONTRACT, preferred_element_type=F32) * c
        top = jnp.max(s, axis=0, keepdims=True)
        w = jnp.exp2(s - top)
        total = jnp.sum(w, axis=0, keepdims=True)
        o = jnp.dot(v, w.astype(BF16), preferred_element_type=F32)
        out[0, e, 0:128, :] = (o / total).astype(BF16)
        out[0, e, 128:144, :] = log_sum_rows(top + jnp.log2(total))


def diag(send, fresh):
    prompts, heads, _, part, _ = fresh[0].shape
    rows = part * len(send)
    return pl.pallas_call(
        diag_body,
        grid=(prompts,),
        in_specs=[pl.BlockSpec((1, heads, 1, part, 128), lambda p: (p, 0, 0, 0, 0))] * len(send)
        + [pl.BlockSpec((1, heads, 2, part, 128), lambda p: (p, 0, 0, 0, 0))] * len(send),
        out_specs=pl.BlockSpec((1, heads, 144, rows), lambda p: (p, 0, 0, 0)),
        out_shape=jax.ShapeDtypeStruct((prompts, heads, 144, rows), BF16),
        compiler_params=pltpu.CompilerParams(
            dimension_semantics=("arbitrary",), vmem_limit_bytes=VMEM
        ),
        cost_estimate=pl.CostEstimate(
            flops=4 * prompts * heads * rows * rows * 128,
            bytes_accessed=4_000_000,
            transcendentals=prompts * heads * rows * rows,
        ),
        name="diag",
    )(*send, *fresh)


def attend_body(info, got_0, got_1, text_k, text_v, out, s_even, s_odd, top_s):
    g = pl.program_id(0)
    got = (got_0, got_1)
    blocks = got_0.shape[0]
    rows = 2 * got_0.shape[2]
    c = 128**-0.5 * LOG2E
    lead = text_k.shape[0] // rows
    tiles = lead + blocks - 1
    groups = [list(range(i, min(i + 4, tiles))) for i in range(0, tiles, 4)]
    if len(groups[-1]) == 1:
        last = groups.pop()
        groups[-1] = groups[-1] + last

    def block_of(b, i):
        return lax.rem(b + 1 + (i - lead), blocks)

    def keys(b, i):
        if i < lead:
            return [text_k[i * rows : (i + 1) * rows, :]]
        return [r[block_of(b, i), 1] for r in got]

    def values(b, i):
        if i < lead:
            return [text_v[:, i * rows : (i + 1) * rows]]
        return [r[block_of(b, i), 2] for r in got]

    def score(b, group, top, s_ref):
        k = jnp.concatenate([x for i in group for x in keys(b, i)], 0)
        q = jnp.concatenate([r[b, 0] for r in got], 0)
        scores = lax.dot_general(k, q, CONTRACT, preferred_element_type=F32)
        for m, i in enumerate(group):
            s = scores[m * rows : (m + 1) * rows, :]
            if i < lead:
                at = i * rows + lax.broadcasted_iota(jnp.int32, s.shape, 0)
                s = jnp.where(at < info[0], s, NEG)
            s_ref[i] = s
            part = jnp.max(s.reshape(rows // 8, 8, rows), axis=0)
            top = part if top is None else jnp.maximum(top, part)
        return top

    def whole_top(top):
        return jnp.broadcast_to(jnp.max(top, axis=0, keepdims=True) * c, (8, rows))

    @pl.when(g == 0)
    def _():
        top = None
        for group in groups:
            top = score(0, group, top, s_even)
        top_s[...] = whole_top(top)

    top = top_s[...]
    for k in range(2):
        b = 2 * g + k
        nxt = lax.rem(b + 1, blocks)
        here, there = (s_even, s_odd) if k == 0 else (s_odd, s_even)
        total = None
        acc = None
        nxt_top = None
        late = None

        def product(acc, late):
            group, w = late
            v = jnp.concatenate([x for i in group for x in values(b, i)], 1)
            o = jnp.dot(v, w, preferred_element_type=F32)
            return o if acc is None else acc + o

        for group in groups:
            nxt_top = score(nxt, group, nxt_top, there)
            w = []
            for i in group:
                x = jnp.exp2(here[i] * c - top[0:1, :])
                part = jnp.sum(x.reshape(rows // 8, 8, rows), axis=0)
                total = part if total is None else total + part
                w.append(x.astype(BF16))
            if late is not None:
                acc = product(acc, late)
            late = (group, jnp.concatenate(w, 0))
        acc = product(acc, late)
        total = jnp.sum(total, axis=0, keepdims=True)
        acc = (acc / total).astype(BF16)
        lse = log_sum_rows(top[0:1, :] + jnp.log2(total))
        for seat in range(2):
            out[k, seat, 0:128, :] = acc
            out[k, seat, 128:144, :] = lse
        top = whole_top(nxt_top)
    top_s[...] = top


def attend(info, got, text_k, text_v):
    blocks, _, part, _ = got[0].shape
    rows = part * len(got)
    tiles = text_k.shape[0] // rows + blocks - 1
    return pl.pallas_call(
        attend_body,
        grid_spec=pltpu.PrefetchScalarGridSpec(
            num_scalar_prefetch=1,
            grid=(blocks // 2,),
            in_specs=[
                pl.BlockSpec(got[0].shape, lambda b, s: (0, 0, 0, 0)),
                pl.BlockSpec(got[1].shape, lambda b, s: (0, 0, 0, 0)),
                pl.BlockSpec(text_k.shape, lambda b, s: (0, 0)),
                pl.BlockSpec(text_v.shape, lambda b, s: (0, 0)),
            ],
            out_specs=pl.BlockSpec((2, 2, 144, rows), lambda b, s: (b, 0, 0, 0)),
            scratch_shapes=[
                pltpu.VMEM((tiles, rows, rows), F32),
                pltpu.VMEM((tiles, rows, rows), F32),
                pltpu.VMEM((8, rows), F32),
            ],
        ),
        out_shape=jax.ShapeDtypeStruct((blocks, 2, 144, rows), BF16),
        compiler_params=pltpu.CompilerParams(
            dimension_semantics=("arbitrary",), vmem_limit_bytes=VMEM
        ),
        cost_estimate=pl.CostEstimate(
            flops=4 * blocks * rows * tiles * rows * 128 * 2,
            bytes_accessed=8_000_000,
            transcendentals=blocks * rows * tiles * rows,
        ),
        name="attend",
    )(info, *got, text_k, text_v)


def project_body(info, got, near, far, w_own, w_oth, gate, hidden, cached, out, all_s):
    n = pl.program_id(0)
    prompts, rows, _ = hidden.shape
    part = w_own.shape[0]
    heads = part // 128
    h = info[0]

    def log_sum(x):
        x = x.astype(F32)
        return x[0:1, :] + x[1:2, :] + x[2:3, :]

    @pl.when(n == 0)
    def _():
        for p in range(prompts):
            for k in range(2):
                own = (near, far)[k]
                seat = h if k == 0 else 1 - h
                for j in range(heads):
                    at = (p * SLOTS + j) * 2 + seat
                    a = log_sum(got[at, 128:144, :])
                    b = log_sum(own[p, j, 128:144, :])
                    high = jnp.maximum(a, b)
                    a, b = jnp.exp2(a - high), jnp.exp2(b - high)
                    o = (got[at, 0:128, :].astype(F32) * a + own[p, j, 0:128, :].astype(F32) * b) / (a + b)
                    col = (k * heads + j) * 128
                    all_s[p * rows : (p + 1) * rows, col : col + 128] = jnp.transpose(o.astype(BF16))

    acc = jnp.dot(all_s[:, 0:part], w_own[...], preferred_element_type=F32)
    acc = acc + jnp.dot(all_s[:, part : 2 * part], w_oth[...], preferred_element_type=F32)
    for p in range(prompts):
        y = hidden[p].astype(F32) + gate[p] * acc[p * rows : (p + 1) * rows, :]
        out[p] = (y + cached[p].astype(F32)).astype(BF16)


def project(info, got, near, far, w_out, w_oth, gate, hidden, cached):
    prompts, rows, width = hidden.shape
    part = w_out.shape[0]
    bn = 512
    steps = width // bn
    return pl.pallas_call(
        project_body,
        grid_spec=pltpu.PrefetchScalarGridSpec(
            num_scalar_prefetch=1,
            grid=(steps,),
            in_specs=[
                pl.BlockSpec(got.shape, lambda n, s: (0, 0, 0)),
                pl.BlockSpec(near.shape, lambda n, s: (0, 0, 0, 0)),
                pl.BlockSpec(far.shape, lambda n, s: (0, 0, 0, 0)),
                pl.BlockSpec((part, bn), lambda n, s: (0, s[0] * steps + n)),
                pl.BlockSpec((part, bn), lambda n, s: (0, n)),
                pl.BlockSpec((prompts, 1, bn), lambda n, s: (0, 0, n)),
                pl.BlockSpec((prompts, rows, bn), lambda n, s: (0, 0, n)),
                pl.BlockSpec((prompts, rows, bn), lambda n, s: (0, 0, n)),
            ],
            out_specs=pl.BlockSpec((prompts, rows, bn), lambda n, s: (0, 0, n)),
            scratch_shapes=[pltpu.VMEM((prompts * rows, 2 * part), BF16)],
        ),
        out_shape=jax.ShapeDtypeStruct((prompts, rows, width), BF16),
        compiler_params=pltpu.CompilerParams(
            dimension_semantics=("arbitrary",), vmem_limit_bytes=VMEM
        ),
        cost_estimate=pl.CostEstimate(
            flops=4 * prompts * rows * part * width, bytes_accessed=12_000_000, transcendentals=0
        ),
        name="project",
    )(info, got, near, far, w_out, w_oth, gate, hidden, cached)


def per_device(
    image_hidden,
    modulation,
    qkv_weight,
    out_weight,
    q_gain,
    k_gain,
    text_keys,
    text_values,
    stale_keys,
    stale_values,
    cached_residual,
    patch_of,
    refresh,
    text_len,
):
    prompts, rows, width_part = image_hidden.shape
    head_dim = q_gain.shape[0]
    channels = out_weight.shape[0]
    heads = channels // head_dim
    seat = lax.axis_index("seq")
    head_seat = lax.axis_index("head")
    batch_seat = lax.axis_index("batch")
    n_seq = lax.axis_size("seq")
    n_batch = lax.axis_size("batch")
    swap = [(0, 1), (1, 0)]

    halves = 2
    half = rows // halves
    other_hidden = []
    for i in range(halves):
        other_hidden.append(lax.ppermute(image_hidden[:, i * half : (i + 1) * half], "head", swap))

    text = jnp.stack([text_keys, text_values], 1)
    t_rows = text.shape[2]
    text = text.reshape(prompts, 2, t_rows, heads, head_dim).transpose(0, 3, 1, 2, 4)
    text = jnp.pad(text, ((0, 0), (0, SLOTS - heads), (0, 0), (0, 0), (0, 0)))
    text = text.reshape(n_seq, 2, t_rows, head_dim)
    text = lax.all_to_all(text, "seq", split_axis=0, concat_axis=0, tiled=True)
    text_k = text[:, 0].reshape(n_seq * t_rows, head_dim)
    text_v = text[:, 1].reshape(n_seq * t_rows, head_dim).T

    n_y = n_seq // 4
    y_seat = seat // 4
    share = channels // (n_batch * n_y)
    piece = lax.dynamic_slice(
        out_weight,
        ((batch_seat * n_y + y_seat) * share, (1 - head_seat) * width_part),
        (share, width_part),
    )
    piece = lax.ppermute(piece, "head", swap)

    seats = jnp.arange(n_seq, dtype=jnp.int32)
    own_band = jnp.sum(jnp.where(seats == seat, patch_of, 0))
    own_flag = jnp.sum(jnp.where(seats == seat, refresh, 0))
    raster = own_band * rows + jnp.arange(rows, dtype=jnp.int32)
    cos, sin = rotary_tables(raster, head_dim, GRID_W)
    info = jnp.stack([head_seat.astype(jnp.int32), own_flag.astype(jnp.int32)])
    mod_view = modulation.transpose(1, 0, 2)
    weight_view = qkv_weight.transpose(1, 0, 2)
    gains = jnp.stack([q_gain, k_gain])
    send, fresh, got = [], [], []
    for i in range(halves):
        s, f = qkv(
            i,
            info,
            image_hidden,
            other_hidden[i],
            mod_view,
            weight_view,
            gains,
            cos,
            sin,
            stale_keys,
            stale_values,
        )
        send.append(s)
        fresh.append(f)
        got.append(
            lax.all_to_all(
                s.reshape(n_seq, 3, half, head_dim), "seq", split_axis=0, concat_axis=0, tiled=True
            )
        )
    piece, _ = lax.optimization_barrier((piece, send[0]))
    w_y = jnp.zeros((n_y, share, width_part), BF16)
    w_y = lax.dynamic_update_slice(w_y, piece[None], (y_seat, 0, 0))
    for d in range(1, n_y):
        moved = lax.ppermute(piece, "seq", [(i, (i + 4 * d) % n_seq) for i in range(n_seq)])
        w_y = lax.dynamic_update_slice(w_y, moved[None], ((y_seat - d) % n_y, 0, 0))
    w_y, _ = lax.optimization_barrier((w_y, send[1]))
    w_oth = jnp.zeros((n_batch, n_y, share, width_part), BF16)
    w_oth = lax.dynamic_update_slice(w_oth, w_y[None], (batch_seat, 0, 0, 0))
    for d in range(1, n_batch):
        moved = lax.ppermute(w_y, "batch", [(i, (i + d) % n_batch) for i in range(n_batch)])
        w_oth = lax.dynamic_update_slice(w_oth, moved[None], ((batch_seat - d) % n_batch, 0, 0, 0))
    w_oth = w_oth.reshape(channels, width_part)
    near = diag(send, fresh)
    got[1], near_sent = lax.optimization_barrier((got[1], near))
    far = lax.ppermute(near_sent, "head", swap)
    unit_prompt = jnp.minimum(seat // SLOTS, prompts - 1)
    length = jnp.sum(jnp.where(jnp.arange(prompts) == unit_prompt, text_len, 0)).astype(jnp.int32)
    back = attend(length[None], got, text_k, text_v)
    back = lax.all_to_all(
        back.reshape(n_seq * 2, 144, rows), ("seq", "head"), split_axis=0, concat_axis=0, tiled=True
    )
    gate = lax.dynamic_slice_in_dim(modulation[:, 2:3], head_seat * width_part, width_part, 2)
    return project(info, back, near, far, out_weight, w_oth, gate, image_hidden, cached_residual)


def solution(mesh):
    in_specs = (
        P("batch", "seq", "head"),
        P("batch", None, None),
        P(None, None, "head"),
        P("head", None),
        P(),
        P(),
        P("batch", "seq", "head"),
        P("batch", "seq", "head"),
        P("batch", "seq", "head"),
        P("batch", "seq", "head"),
        P("batch", "seq", "head"),
        P("batch"),
        P("batch"),
        P("batch"),
    )
    out_specs = P("batch", "seq", "head")
    return jax.shard_map(
        per_device, mesh=mesh, in_specs=in_specs, out_specs=out_specs, check_vma=False
    )
```

profile of v0, /device:TPU:0, one launch (start us, length us, event | category | flops | bytes accessed | tf_op | source)
XLA Modules:
  0.0 219.8 jit_solution(615593993493865836)
XLA Ops:
  0.0 1.5 fusion.14
  1.6 3.3 %collective-permute-start.1 = (bf16[2,128,1536]{2,1,0:T(8,128)(2,1)S(1)}, bf16[2,128,1536]{2,1,0:T(8,128)(2,1)S(1)}, u32[]{:S(2)}, u32[]{:S(2)}) collective-permute-start(bf16[2,128,1536]{2,1,0:T(8,128)(2,1)S(1)} %get-tuple-element.21), channel_id=1, source_target_pairs={{0,1},{1,0},{2,3},{3,2},{4,5},{5,4},{6,7},{7,6},{8,9},{9,8},{10,11... | collective-permute-start | bytes 2359304 | tf_op jit(solution)/shard_map/ppermute | solution.py:441
  5.2 0.7 pad.4.clone
  6.0 4.6 %all-to-all-start.2 = ((bf16[16,2,32,128]{3,2,1,0:T(8,128)(2,1)}), bf16[16,2,32,128]{3,2,1,0:T(8,128)(2,1)S(1)}, u32[]{:S(2)}, u32[]{:S(2)}) async-start(bf16[16,2,32,128]{3,2,1,0:T(8,128)(2,1)} %bitcast.10), calls=%async_computation.2 | async-start | bytes 524288 | tf_op jit(solution)/shard_map/all_to_all | solution.py:448
  10.6 0.6 fusion.11
  11.3 0.7 fusion.12
  12.6 1.3 pad_add_fusion.info
  13.9 0.5 pad_maximum_fusion.2.gains
  14.5 0.5 fusion.2
  15.1 0.8 pad_maximum_fusion.cos
  15.8 0.8 pad_maximum_fusion.1.sin
  16.6 7.0 %collective-permute-done.1.oth = bf16[2,128,1536]{2,1,0:T(8,128)(2,1)S(1)} collective-permute-done((bf16[2,128,1536]{2,1,0:T(8,128)(2,1)S(1)}, bf16[2,128,1536]{2,1,0:T(8,128)(2,1)S(1)}, u32[]{:S(2)}, u32[]{:S(2)}) %collective-permute-start.1) | collective-permute-done | bytes 786464 | tf_op jit(solution)/shard_map/ppermute | solution.py:441
  23.6 0.9 copy-done.5
  24.4 11.9 %qkv.3 = (bf16[2,8,3,128,128]{4,3,2,1,0:T(8,128)(2,1)}, bf16[2,6,2,128,128]{4,3,2,1,0:T(8,128)(2,1)}) custom-call(s32[2]{0:T(128)} %pad_add_fusion.info, bf16[2,256,1536]{2,1,0:T(8,128)(2,1)} %hidden.1, bf16[2,128,1536]{2,1,0:T(8,128)(2,1)} %copy-done.5, f32[3,2,3072]{2,1,0:T(2,128)} %bitcast.41, f32[3,2,3072]{2,1,0:T(2,128)} %bitcast.42, ...), custom_call_target="tpu_custom_call" | custom-call | flops 3623878656 | bytes 20000000 | tf_op jit(solution)/shard_map/qkv/pallas_call | solution.py:125
  36.3 5.7 %all-to-all-start.1 = ((bf16[16,3,128,128]{3,2,1,0:T(8,128)(2,1)}), bf16[16,3,128,128]{3,2,1,0:T(8,128)(2,1)S(1)}, u32[]{:S(2)}, u32[]{:S(2)}) async-start(bf16[16,3,128,128]{3,2,1,0:T(8,128)(2,1)} %bitcast.38), calls=%async_computation.1 | async-start | bytes 3145728 | tf_op jit(solution)/shard_map/all_to_all | solution.py:489
  42.0 2.8 %collective-permute-start = (bf16[2,128,1536]{2,1,0:T(8,128)(2,1)S(1)}, bf16[2,128,1536]{2,1,0:T(8,128)(2,1)S(1)}, u32[]{:S(2)}, u32[]{:S(2)}) collective-permute-start(bf16[2,128,1536]{2,1,0:T(8,128)(2,1)S(1)} %get-tuple-element.22), channel_id=1, source_target_pairs={{0,1},{1,0},{2,3},{3,2},{4,5},{5,4},{6,7},{7,6},{8,9},{9,8},{10,11... | collective-permute-start | bytes 2359304 | tf_op jit(solution)/shard_map/ppermute | solution.py:441
  44.8 1.6 dynamic_slice.6
  46.4 0.8 collective-permute-start.3
  47.2 1.3 slice.19
  48.6 1.3 fusion.13
  49.9 31.4 %collective-permute-done.oth = bf16[2,128,1536]{2,1,0:T(8,128)(2,1)S(1)} collective-permute-done((bf16[2,128,1536]{2,1,0:T(8,128)(2,1)S(1)}, bf16[2,128,1536]{2,1,0:T(8,128)(2,1)S(1)}, u32[]{:S(2)}, u32[]{:S(2)}) %collective-permute-start) | collective-permute-done | bytes 786464 | tf_op jit(solution)/shard_map/ppermute | solution.py:441
  81.3 0.9 copy-done.4
  82.2 11.9 %qkv.2 = (bf16[2,8,3,128,128]{4,3,2,1,0:T(8,128)(2,1)}, bf16[2,6,2,128,128]{4,3,2,1,0:T(8,128)(2,1)}) custom-call(s32[2]{0:T(128)} %pad_add_fusion.info, bf16[2,256,1536]{2,1,0:T(8,128)(2,1)} %hidden.1, bf16[2,128,1536]{2,1,0:T(8,128)(2,1)} %copy-done.4, f32[3,2,3072]{2,1,0:T(2,128)} %bitcast.43, f32[3,2,3072]{2,1,0:T(2,128)} %bitcast.44, ...), custom_call_target="tpu_custom_call" | custom-call | flops 3623878656 | bytes 20000000 | tf_op jit(solution)/shard_map/qkv/pallas_call | solution.py:125
  94.1 4.7 %all-to-all-start = ((bf16[16,3,128,128]{3,2,1,0:T(8,128)(2,1)}), bf16[16,3,128,128]{3,2,1,0:T(8,128)(2,1)}, u32[]{:S(2)}, u32[]{:S(2)}) async-start(bf16[16,3,128,128]{3,2,1,0:T(8,128)(2,1)} %bitcast.39), calls=%async_computation | async-start | bytes 3145728 | tf_op jit(solution)/shard_map/all_to_all | solution.py:489
  98.8 0.7 fusion.15
  99.4 0.8 copy.21
  100.2 1.9 collective-permute-start.4
  102.1 2.7 %collective-permute-start.5 = (bf16[48,1536]{1,0:T(8,128)(2,1)S(1)}, bf16[48,1536]{1,0:T(8,128)(2,1)S(1)}, u32[]{:S(2)}, u32[]{:S(2)}) collective-permute-start(bf16[48,1536]{1,0:T(8,128)(2,1)S(1)} %collective-permute-done.3), channel_id=1, source_target_pairs={{0,16},{2,18},{4,20},{6,22},{8,24},{10,26},{12,28},{14,30},{16,0},... | collective-permute-start | bytes 442376 | tf_op jit(solution)/shard_map/ppermute | solution.py:497
  104.8 1.5 collective-permute-start.6
  106.3 5.9 %diag.1.near = bf16[2,6,144,256]{3,2,1,0:T(8,128)(2,1)} custom-call(bf16[2,8,3,128,128]{4,3,2,1,0:T(8,128)(2,1)} %get-tuple-element.13.refs_0_, bf16[2,8,3,128,128]{4,3,2,1,0:T(8,128)(2,1)} %get-tuple-element.14.refs_1_, bf16[2,6,2,128,128]{4,3,2,1,0:T(8,128)(2,1)} %get-tuple-element.15.refs_2_, bf16[2,6,2,128,128]{4,3,2,1,0:T(8,128)(2,1)} %get-tuple-element.16.refs_3_), custom_call_target="tpu_custom_call" | custom-call | flops 402653184 | bytes 4000000 | tf_op jit(solution)/shard_map/diag/pallas_call | solution.py:200
  112.2 11.1 %collective-permute-done.4 = bf16[48,1536]{1,0:T(8,128)(2,1)S(1)} collective-permute-done((bf16[48,1536]{1,0:T(8,128)(2,1)S(1)}, bf16[48,1536]{1,0:T(8,128)(2,1)S(1)}, u32[]{:S(2)}, u32[]{:S(2)}) %collective-permute-start.4) | collective-permute-done | bytes 147488 | tf_op jit(solution)/shard_map/ppermute | solution.py:497
  123.3 3.2 %collective-permute-done.5 = bf16[48,1536]{1,0:T(8,128)(2,1)S(1)} collective-permute-done((bf16[48,1536]{1,0:T(8,128)(2,1)S(1)}, bf16[48,1536]{1,0:T(8,128)(2,1)S(1)}, u32[]{:S(2)}, u32[]{:S(2)}) %collective-permute-start.5) | collective-permute-done | bytes 147488 | tf_op jit(solution)/shard_map/ppermute | solution.py:497
  126.5 28.0 %attend.1 = bf16[16,2,144,256]{3,2,1,0:T(8,128)(2,1)} custom-call(s32[1]{0:T(128)} %bitcast.2.info, bf16[16,3,128,128]{3,2,1,0:T(8,128)(2,1)} %all-to-all-done.got_0, bf16[16,3,128,128]{3,2,1,0:T(8,128)(2,1)} %copy-done.3, bf16[512,128]{1,0:T(8,128)(2,1)} %bitcast.47, bf16[128,512]{1,0:T(8,128)(2,1)} %bitcast.46), custom_call_target="tpu_custom_call" | custom-call | flops 18253611008 | bytes 8000000 | tf_op jit(solution)/shard_map/attend/pallas_call | solution.py:311
  154.5 4.1 %all-to-all-start.3 = ((bf16[32,144,256]{2,1,0:T(8,128)(2,1)}), bf16[32,144,256]{2,1,0:T(8,128)(2,1)S(1)}, u32[]{:S(2)}, u32[]{:S(2)}) async-start(bf16[32,144,256]{2,1,0:T(8,128)(2,1)} %bitcast.40), calls=%async_computation.3 | async-start | bytes 4718592 | tf_op jit(solution)/shard_map/all_to_all | solution.py:512
  158.6 2.0 collective-permute-start.7
  160.6 0.7 constant_dynamic-slice_fusion
  161.3 0.6 copy.23.gate
  161.9 3.5 %collective-permute-start.8 = (bf16[4,48,1536]{2,1,0:T(8,128)(2,1)S(1)}, bf16[4,48,1536]{2,1,0:T(8,128)(2,1)S(1)}, u32[]{:S(2)}, u32[]{:S(2)}) collective-permute-start(bf16[4,48,1536]{2,1,0:T(8,128)(2,1)S(1)} %bitcast_dynamic-update-slice_fusion.4), channel_id=1, source_target_pairs={{0,64},{32,96},{64,0},{96,32},{1,65},{33,97},{65,1},{97,33},{2,66}... | collective-permute-start | bytes 1769480 | tf_op jit(solution)/shard_map/ppermute | solution.py:503
  165.5 1.0 collective-permute-start.9
  166.5 0.2 broadcast_in_dim.81
  166.8 9.6 %collective-permute-done.7 = bf16[4,48,1536]{2,1,0:T(8,128)(2,1)S(1)} collective-permute-done((bf16[4,48,1536]{2,1,0:T(8,128)(2,1)S(1)}, bf16[4,48,1536]{2,1,0:T(8,128)(2,1)S(1)}, u32[]{:S(2)}, u32[]{:S(2)}) %collective-permute-start.7) | collective-permute-done | bytes 589856 | tf_op jit(solution)/shard_map/ppermute | solution.py:503
  176.4 3.2 %collective-permute-start.2 = (bf16[2,6,144,256]{3,2,1,0:T(8,128)(2,1)S(1)}, bf16[2,6,144,256]{3,2,1,0:T(8,128)(2,1)}, u32[]{:S(2)}, u32[]{:S(2)}) collective-permute-start(bf16[2,6,144,256]{3,2,1,0:T(8,128)(2,1)S(1)} %copy-done.2), channel_id=1, source_target_pairs={{0,1},{1,0},{2,3},{3,2},{4,5},{5,4},{6,7},{7,6},{8,9},{9,8},{10,11... | collective-permute-start | bytes 2654216 | tf_op jit(solution)/shard_map/ppermute | solution.py:508
  179.6 10.5 %collective-permute-done.8 = bf16[4,48,1536]{2,1,0:T(8,128)(2,1)S(1)} collective-permute-done((bf16[4,48,1536]{2,1,0:T(8,128)(2,1)S(1)}, bf16[4,48,1536]{2,1,0:T(8,128)(2,1)S(1)}, u32[]{:S(2)}, u32[]{:S(2)}) %collective-permute-start.8) | collective-permute-done | bytes 589856 | tf_op jit(solution)/shard_map/ppermute | solution.py:503
  190.2 0.7 collective-permute-done.9
  191.0 1.4 copy-done.1
  192.4 16.2 %collective-permute-done.2.far = bf16[2,6,144,256]{3,2,1,0:T(8,128)(2,1)} collective-permute-done((bf16[2,6,144,256]{3,2,1,0:T(8,128)(2,1)S(1)}, bf16[2,6,144,256]{3,2,1,0:T(8,128)(2,1)}, u32[]{:S(2)}, u32[]{:S(2)}) %collective-permute-start.2) | collective-permute-done | bytes 884768 | tf_op jit(solution)/shard_map/ppermute | solution.py:508
  208.6 1.4 copy-done
  210.1 9.8 %project.1 = bf16[2,256,1536]{2,1,0:T(8,128)(2,1)} custom-call(s32[2]{0:T(128)} %pad_add_fusion.info, bf16[32,144,256]{2,1,0:T(8,128)(2,1)} %copy-done, bf16[2,6,144,256]{3,2,1,0:T(8,128)(2,1)} %diag.1.near, bf16[2,6,144,256]{3,2,1,0:T(8,128)(2,1)} %collective-permute-done.2.far, bf16[768,3072]{1,0:T(8,128)(2,1)} %w_own.1, bf16[768,1536]{1,0:T(8,128)(2,1)} %bitcast.37, ...), custom_call_target="tpu_custom_call" | custom-call | flops 2415919104 | bytes 12000000 | tf_op jit(solution)/shard_map/project/pallas_call | solution.py:381
  (42 shorter events, 0.7 us)
Async XLA Ops:
  0.0 4.8 %copy-start.6 = (bf16[2,32,768]{2,1,0:T(8,128)(2,1)S(1)}, bf16[2,32,768]{2,1,0:T(8,128)(2,1)}, u32[]{:S(2)}) copy-start(bf16[2,32,768]{2,1,0:T(8,128)(2,1)} %param.21) | copy-start | bytes 294916
  0.0 5.0 %copy-start.7 = (bf16[2,32,768]{2,1,0:T(8,128)(2,1)S(1)}, bf16[2,32,768]{2,1,0:T(8,128)(2,1)}, u32[]{:S(2)}) copy-start(bf16[2,32,768]{2,1,0:T(8,128)(2,1)} %param.20) | copy-start | bytes 294916
  0.0 10.6 %copy-start.10 = (s32[16]{0:T(128)S(1)}, s32[16]{0:T(128)}, u32[]{:S(2)}) copy-start(s32[16]{0:T(128)} %param.26) | copy-start | bytes 196
  0.0 11.3 %copy-start.11 = (s32[16]{0:T(128)S(1)}, s32[16]{0:T(128)}, u32[]{:S(2)}) copy-start(s32[16]{0:T(128)} %param.25) | copy-start | bytes 196
  0.0 13.9 %copy-start.8 = (f32[128]{0:T(128)S(1)}, f32[128]{0:T(128)}, u32[]{:S(2)}) copy-start(f32[128]{0:T(128)} %param.19) | copy-start | bytes 1540
  0.0 13.9 %copy-start.9 = (f32[128]{0:T(128)S(1)}, f32[128]{0:T(128)}, u32[]{:S(2)}) copy-start(f32[128]{0:T(128)} %param.18) | copy-start | bytes 1540
  1.6 22.0 %collective-permute-start.1 = (bf16[2,128,1536]{2,1,0:T(8,128)(2,1)S(1)}, bf16[2,128,1536]{2,1,0:T(8,128)(2,1)S(1)}, u32[]{:S(2)}, u32[]{:S(2)}) collective-permute-start(bf16[2,128,1536]{2,1,0:T(8,128)(2,1)S(1)} %get-tuple-element.21), channel_id=1, source_target_pairs={{0,1},{1,0},{2,3},{3,2},{4,5},{5,4},{6,7},{7,6},{8,9},{9,8},{10,11... | collective-permute-start | bytes 2359304 | tf_op jit(solution)/shard_map/ppermute | solution.py:441
  6.0 30.4 %all-to-all-start.2 = ((bf16[16,2,32,128]{3,2,1,0:T(8,128)(2,1)}), bf16[16,2,32,128]{3,2,1,0:T(8,128)(2,1)S(1)}, u32[]{:S(2)}, u32[]{:S(2)}) async-start(bf16[16,2,32,128]{3,2,1,0:T(8,128)(2,1)} %bitcast.10), calls=%async_computation.2 | async-start | bytes 524288 | tf_op jit(solution)/shard_map/all_to_all | solution.py:448
  23.6 0.9 copy-start.5
  36.3 57.7 %all-to-all-start.1 = ((bf16[16,3,128,128]{3,2,1,0:T(8,128)(2,1)}), bf16[16,3,128,128]{3,2,1,0:T(8,128)(2,1)S(1)}, u32[]{:S(2)}, u32[]{:S(2)}) async-start(bf16[16,3,128,128]{3,2,1,0:T(8,128)(2,1)} %bitcast.38), calls=%async_computation.1 | async-start | bytes 3145728 | tf_op jit(solution)/shard_map/all_to_all | solution.py:489
  42.0 39.2 %collective-permute-start = (bf16[2,128,1536]{2,1,0:T(8,128)(2,1)S(1)}, bf16[2,128,1536]{2,1,0:T(8,128)(2,1)S(1)}, u32[]{:S(2)}, u32[]{:S(2)}) collective-permute-start(bf16[2,128,1536]{2,1,0:T(8,128)(2,1)S(1)} %get-tuple-element.22), channel_id=1, source_target_pairs={{0,1},{1,0},{2,3},{3,2},{4,5},{5,4},{6,7},{7,6},{8,9},{9,8},{10,11... | collective-permute-start | bytes 2359304 | tf_op jit(solution)/shard_map/ppermute | solution.py:441
  46.4 53.8 %collective-permute-start.3 = (bf16[48,1536]{1,0:T(8,128)(2,1)}, bf16[48,1536]{1,0:T(8,128)(2,1)S(1)}, u32[]{:S(2)}, u32[]{:S(2)}) collective-permute-start(bf16[48,1536]{1,0:T(8,128)(2,1)} %dynamic_slice.6), channel_id=1, source_target_pairs={{0,1},{1,0},{2,3},{3,2},{4,5},{5,4},{6,7},{7,6},{8,9},{9,8},{10,11... | collective-permute-start | bytes 442376 | tf_op jit(solution)/shard_map/ppermute | solution.py:460
  81.3 0.9 copy-start.4
  94.1 12.2 %copy-start.3 = (bf16[16,3,128,128]{3,2,1,0:T(8,128)(2,1)}, bf16[16,3,128,128]{3,2,1,0:T(8,128)(2,1)S(1)}, u32[]{:S(2)}) copy-start(bf16[16,3,128,128]{3,2,1,0:T(8,128)(2,1)S(1)} %all-to-all-done.1.got_1) | copy-start | bytes 4718596
  94.1 32.4 %all-to-all-start = ((bf16[16,3,128,128]{3,2,1,0:T(8,128)(2,1)}), bf16[16,3,128,128]{3,2,1,0:T(8,128)(2,1)}, u32[]{:S(2)}, u32[]{:S(2)}) async-start(bf16[16,3,128,128]{3,2,1,0:T(8,128)(2,1)} %bitcast.39), calls=%async_computation | async-start | bytes 3145728 | tf_op jit(solution)/shard_map/all_to_all | solution.py:489
  100.2 23.1 %collective-permute-start.4 = (bf16[48,1536]{1,0:T(8,128)(2,1)S(1)}, bf16[48,1536]{1,0:T(8,128)(2,1)S(1)}, u32[]{:S(2)}, u32[]{:S(2)}) collective-permute-start(bf16[48,1536]{1,0:T(8,128)(2,1)S(1)} %collective-permute-done.3), channel_id=1, source_target_pairs={{0,8},{2,10},{4,12},{6,14},{8,16},{10,18},{12,20},{14,22},{16,24},... | collective-permute-start | bytes 442376 | tf_op jit(solution)/shard_map/ppermute | solution.py:497
  102.1 24.4 %collective-permute-start.5 = (bf16[48,1536]{1,0:T(8,128)(2,1)S(1)}, bf16[48,1536]{1,0:T(8,128)(2,1)S(1)}, u32[]{:S(2)}, u32[]{:S(2)}) collective-permute-start(bf16[48,1536]{1,0:T(8,128)(2,1)S(1)} %collective-permute-done.3), channel_id=1, source_target_pairs={{0,16},{2,18},{4,20},{6,22},{8,24},{10,26},{12,28},{14,30},{16,0},... | collective-permute-start | bytes 442376 | tf_op jit(solution)/shard_map/ppermute | solution.py:497
  104.8 53.8 %collective-permute-start.6 = (bf16[48,1536]{1,0:T(8,128)(2,1)S(1)}, bf16[48,1536]{1,0:T(8,128)(2,1)S(1)}, u32[]{:S(2)}, u32[]{:S(2)}) collective-permute-start(bf16[48,1536]{1,0:T(8,128)(2,1)S(1)} %collective-permute-done.3), channel_id=1, source_target_pairs={{0,24},{2,26},{4,28},{6,30},{8,0},{10,2},{12,4},{14,6},{16,8},{18,... | collective-permute-start | bytes 442376 | tf_op jit(solution)/shard_map/ppermute | solution.py:497
  154.5 54.1 %all-to-all-start.3 = ((bf16[32,144,256]{2,1,0:T(8,128)(2,1)}), bf16[32,144,256]{2,1,0:T(8,128)(2,1)S(1)}, u32[]{:S(2)}, u32[]{:S(2)}) async-start(bf16[32,144,256]{2,1,0:T(8,128)(2,1)} %bitcast.40), calls=%async_computation.3 | async-start | bytes 4718592 | tf_op jit(solution)/shard_map/all_to_all | solution.py:512
  158.6 17.7 %collective-permute-start.7 = (bf16[4,48,1536]{2,1,0:T(8,128)(2,1)S(1)}, bf16[4,48,1536]{2,1,0:T(8,128)(2,1)S(1)}, u32[]{:S(2)}, u32[]{:S(2)}) collective-permute-start(bf16[4,48,1536]{2,1,0:T(8,128)(2,1)S(1)} %bitcast_dynamic-update-slice_fusion.4), channel_id=1, source_target_pairs={{0,32},{32,64},{64,96},{96,0},{1,33},{33,65},{65,97},{97,1},{2,34}... | collective-permute-start | bytes 1769480 | tf_op jit(solution)/shard_map/ppermute | solution.py:503
  161.9 14.5 %copy-start.2 = (bf16[2,6,144,256]{3,2,1,0:T(8,128)(2,1)S(1)}, bf16[2,6,144,256]{3,2,1,0:T(8,128)(2,1)}, u32[]{:S(2)}) copy-start(bf16[2,6,144,256]{3,2,1,0:T(8,128)(2,1)} %diag.1.near) | copy-start | bytes 2654212
  161.9 28.2 %collective-permute-start.8 = (bf16[4,48,1536]{2,1,0:T(8,128)(2,1)S(1)}, bf16[4,48,1536]{2,1,0:T(8,128)(2,1)S(1)}, u32[]{:S(2)}, u32[]{:S(2)}) collective-permute-start(bf16[4,48,1536]{2,1,0:T(8,128)(2,1)S(1)} %bitcast_dynamic-update-slice_fusion.4), channel_id=1, source_target_pairs={{0,64},{32,96},{64,0},{96,32},{1,65},{33,97},{65,1},{97,33},{2,66}... | collective-permute-start | bytes 1769480 | tf_op jit(solution)/shard_map/ppermute | solution.py:503
  165.5 25.5 %collective-permute-start.9 = (bf16[4,48,1536]{2,1,0:T(8,128)(2,1)S(1)}, bf16[4,48,1536]{2,1,0:T(8,128)(2,1)S(1)}, u32[]{:S(2)}, u32[]{:S(2)}) collective-permute-start(bf16[4,48,1536]{2,1,0:T(8,128)(2,1)S(1)} %bitcast_dynamic-update-slice_fusion.4), channel_id=1, source_target_pairs={{0,96},{32,0},{64,32},{96,64},{1,97},{33,1},{65,33},{97,65},{2,98}... | collective-permute-start | bytes 1769480 | tf_op jit(solution)/shard_map/ppermute | solution.py:503
  176.4 32.2 %collective-permute-start.2 = (bf16[2,6,144,256]{3,2,1,0:T(8,128)(2,1)S(1)}, bf16[2,6,144,256]{3,2,1,0:T(8,128)(2,1)}, u32[]{:S(2)}, u32[]{:S(2)}) collective-permute-start(bf16[2,6,144,256]{3,2,1,0:T(8,128)(2,1)S(1)} %copy-done.2), channel_id=1, source_target_pairs={{0,1},{1,0},{2,3},{3,2},{4,5},{5,4},{6,7},{7,6},{8,9},{9,8},{10,11... | collective-permute-start | bytes 2654216 | tf_op jit(solution)/shard_map/ppermute | solution.py:508
  191.0 1.4 copy-start.1
  208.6 1.4 copy-start
where the time goes:
time: 221 us; the launch traced here: 220 us
  waiting for transfers between devices  89.7 us (41%)
  Pallas kernels  67.4 us (30%)
  starting transfers between devices  41.8 us (19%)
  local copies, waits for them, and re-layouts  13.4 us (6%)
  other arithmetic  6.65 us (3%)
    ppermute x2, waiting for transfers between devices, per_device(): lax.ppermute(image_hidden[:, i * half:(i + 1) * half], 'head', swap)  38.4 us
    pallas_call x1, Pallas kernels, attend(): pl.pallas_call(attend_body, grid_spec=pltpu.PrefetchScalarGridSpec(num_sc...  28 us
    pallas_call x2, Pallas kernels, qkv(): pl.pallas_call(qkv_body, grid_spec=pltpu.PrefetchScalarGridSpec(num_scala...  23.8 us
    ppermute x3, waiting for transfers between devices, per_device(): lax.ppermute(w_y, 'batch', [(i, (i + d) % n_batch) for i in range(n_batch)])  20.8 us
    ppermute x1, waiting for transfers between devices, per_device(): far = lax.ppermute(near_sent, 'head', swap)  16.2 us
    ppermute x3, waiting for transfers between devices, per_device(): lax.ppermute(piece, 'seq', [(i, (i + 4 * d) % n_seq) for i in range(n_seq)])  14.3 us
    all_to_all x2, starting transfers between devices, per_device(): lax.all_to_all(s.reshape(n_seq, 3, half, head_dim), 'seq', split_axis=0,...  10.4 us
    pallas_call x1, Pallas kernels, project(): pl.pallas_call(project_body, grid_spec=pltpu.PrefetchScalarGridSpec(num_s...  9.76 us
  transfers between devices with their start and end apart: 14, of which 8 were waited for; matrix products, arithmetic and copies ran while one was open for 6% of the time, Pallas kernels for 26%

commit v1 on v0

--- a/solution.py
+++ b/solution.py
@@ -242,10 +242,14 @@
             return [text_v[:, i * rows : (i + 1) * rows]]
         return [r[block_of(b, i), 2] for r in got]
 
-    def score(b, group, top, s_ref):
+    def queries(b):
+        q = jnp.concatenate([r[b, 0] for r in got], 0).astype(F32) * c
+        high = q.astype(BF16)
+        return jnp.concatenate([high, (q - high.astype(F32)).astype(BF16)], 1)
+
+    def score(b, q, group, top, s_ref):
         k = jnp.concatenate([x for i in group for x in keys(b, i)], 0)
-        q = jnp.concatenate([r[b, 0] for r in got], 0)
-        scores = lax.dot_general(k, q, CONTRACT, preferred_element_type=F32)
+        scores = lax.dot_general(jnp.concatenate([k, k], 1), q, CONTRACT, preferred_element_type=F32)
         for m, i in enumerate(group):
             s = scores[m * rows : (m + 1) * rows, :]
             if i < lead:
@@ -257,13 +261,14 @@
         return top
 
     def whole_top(top):
-        return jnp.broadcast_to(jnp.max(top, axis=0, keepdims=True) * c, (8, rows))
+        return jnp.broadcast_to(jnp.max(top, axis=0, keepdims=True), (8, rows))
 
     @pl.when(g == 0)
     def _():
         top = None
+        q = queries(0)
         for group in groups:
-            top = score(0, group, top, s_even)
+            top = score(0, q, group, top, s_even)
         top_s[...] = whole_top(top)
 
     top = top_s[...]
@@ -275,6 +280,7 @@
         acc = None
         nxt_top = None
         late = None
+        q = queries(nxt)
 
         def product(acc, late):
             group, w = late
@@ -283,13 +289,13 @@
             return o if acc is None else acc + o
 
         for group in groups:
-            nxt_top = score(nxt, group, nxt_top, there)
+            nxt_top = score(nxt, q, group, nxt_top, there)
             w = []
             for i in group:
-                x = jnp.exp2(here[i] * c - top[0:1, :])
-                part = jnp.sum(x.reshape(rows // 8, 8, rows), axis=0)
+                x = jnp.exp2(here[i].reshape(rows // 8, 8, rows) - top[None])
+                part = jnp.sum(x, axis=0)
                 total = part if total is None else total + part
-                w.append(x.astype(BF16))
+                w.append(x.reshape(rows, rows).astype(BF16))
             if late is not None:
                 acc = product(acc, late)
             late = (group, jnp.concatenate(w, 0))

time: 221 us -> 219 us (level)
  no operation moved by 1% of the time
where the time goes in v1:
time: 219 us; the launch traced here: 218 us
  waiting for transfers between devices  89.7 us (41%)
  Pallas kernels  65.7 us (30%)
  starting transfers between devices  41.8 us (19%)
  local copies, waits for them, and re-layouts  13.4 us (6%)
  other arithmetic  6.65 us (3%)
    ppermute x2, waiting for transfers between devices, per_device(): lax.ppermute(image_hidden[:, i * half:(i + 1) * half], 'head', swap)  38.4 us
    pallas_call x1, Pallas kernels, attend(): pl.pallas_call(attend_body, grid_spec=pltpu.PrefetchScalarGridSpec(num_sc...  26.3 us
    pallas_call x2, Pallas kernels, qkv(): pl.pallas_call(qkv_body, grid_spec=pltpu.PrefetchScalarGridSpec(num_scala...  23.8 us
    ppermute x3, waiting for transfers between devices, per_device(): lax.ppermute(w_y, 'batch', [(i, (i + d) % n_batch) for i in range(n_batch)])  20.9 us
    ppermute x1, waiting for transfers between devices, per_device(): far = lax.ppermute(near_sent, 'head', swap)  16.1 us
    ppermute x3, waiting for transfers between devices, per_device(): lax.ppermute(piece, 'seq', [(i, (i + 4 * d) % n_seq) for i in range(n_seq)])  14.3 us
    all_to_all x2, starting transfers between devices, per_device(): lax.all_to_all(s.reshape(n_seq, 3, half, head_dim), 'seq', split_axis=0,...  10.4 us
    pallas_call x1, Pallas kernels, project(): pl.pallas_call(project_body, grid_spec=pltpu.PrefetchScalarGridSpec(num_s...  9.76 us
  transfers between devices with their start and end apart: 14, of which 8 were waited for; matrix products, arithmetic and copies ran while one was open for 6% of the time, Pallas kernels for 26%

profile of v1, /device:TPU:0, one launch (start us, length us, event | category | flops | bytes accessed | tf_op | source)
XLA Modules:
  0.0 218.2 jit_solution(12924644664934642854)
XLA Ops:
  0.0 1.5 fusion.14
  1.6 3.3 %collective-permute-start.1 = (bf16[2,128,1536]{2,1,0:T(8,128)(2,1)S(1)}, bf16[2,128,1536]{2,1,0:T(8,128)(2,1)S(1)}, u32[]{:S(2)}, u32[]{:S(2)}) collective-permute-start(bf16[2,128,1536]{2,1,0:T(8,128)(2,1)S(1)} %get-tuple-element.21), channel_id=1, source_target_pairs={{0,1},{1,0},{2,3},{3,2},{4,5},{5,4},{6,7},{7,6},{8,9},{9,8},{10,11... | collective-permute-start | bytes 2359304 | tf_op jit(solution)/shard_map/ppermute | solution.py:447
  5.2 0.7 pad.4.clone
  6.0 4.6 %all-to-all-start.2 = ((bf16[16,2,32,128]{3,2,1,0:T(8,128)(2,1)}), bf16[16,2,32,128]{3,2,1,0:T(8,128)(2,1)S(1)}, u32[]{:S(2)}, u32[]{:S(2)}) async-start(bf16[16,2,32,128]{3,2,1,0:T(8,128)(2,1)} %bitcast.10), calls=%async_computation.2 | async-start | bytes 524288 | tf_op jit(solution)/shard_map/all_to_all | solution.py:454
  10.6 0.6 fusion.11
  11.3 0.7 fusion.12
  12.6 1.3 pad_add_fusion.info
  13.9 0.5 pad_maximum_fusion.2.gains
  14.5 0.5 fusion.2
  15.1 0.8 pad_maximum_fusion.cos
  15.8 0.8 pad_maximum_fusion.1.sin
  16.6 7.0 %collective-permute-done.1.oth = bf16[2,128,1536]{2,1,0:T(8,128)(2,1)S(1)} collective-permute-done((bf16[2,128,1536]{2,1,0:T(8,128)(2,1)S(1)}, bf16[2,128,1536]{2,1,0:T(8,128)(2,1)S(1)}, u32[]{:S(2)}, u32[]{:S(2)}) %collective-permute-start.1) | collective-permute-done | bytes 786464 | tf_op jit(solution)/shard_map/ppermute | solution.py:447
  23.6 0.9 copy-done.5
  24.4 11.9 %qkv.3 = (bf16[2,8,3,128,128]{4,3,2,1,0:T(8,128)(2,1)}, bf16[2,6,2,128,128]{4,3,2,1,0:T(8,128)(2,1)}) custom-call(s32[2]{0:T(128)} %pad_add_fusion.info, bf16[2,256,1536]{2,1,0:T(8,128)(2,1)} %hidden.1, bf16[2,128,1536]{2,1,0:T(8,128)(2,1)} %copy-done.5, f32[3,2,3072]{2,1,0:T(2,128)} %bitcast.41, f32[3,2,3072]{2,1,0:T(2,128)} %bitcast.42, ...), custom_call_target="tpu_custom_call" | custom-call | flops 3623878656 | bytes 20000000 | tf_op jit(solution)/shard_map/qkv/pallas_call | solution.py:125
  36.3 5.7 %all-to-all-start.1 = ((bf16[16,3,128,128]{3,2,1,0:T(8,128)(2,1)}), bf16[16,3,128,128]{3,2,1,0:T(8,128)(2,1)S(1)}, u32[]{:S(2)}, u32[]{:S(2)}) async-start(bf16[16,3,128,128]{3,2,1,0:T(8,128)(2,1)} %bitcast.38), calls=%async_computation.1 | async-start | bytes 3145728 | tf_op jit(solution)/shard_map/all_to_all | solution.py:495
  42.0 2.8 %collective-permute-start = (bf16[2,128,1536]{2,1,0:T(8,128)(2,1)S(1)}, bf16[2,128,1536]{2,1,0:T(8,128)(2,1)S(1)}, u32[]{:S(2)}, u32[]{:S(2)}) collective-permute-start(bf16[2,128,1536]{2,1,0:T(8,128)(2,1)S(1)} %get-tuple-element.22), channel_id=1, source_target_pairs={{0,1},{1,0},{2,3},{3,2},{4,5},{5,4},{6,7},{7,6},{8,9},{9,8},{10,11... | collective-permute-start | bytes 2359304 | tf_op jit(solution)/shard_map/ppermute | solution.py:447
  44.8 1.6 dynamic_slice.6
  46.4 0.8 collective-permute-start.3
  47.2 1.3 slice.19
  48.6 1.3 fusion.13
  49.9 31.4 %collective-permute-done.oth = bf16[2,128,1536]{2,1,0:T(8,128)(2,1)S(1)} collective-permute-done((bf16[2,128,1536]{2,1,0:T(8,128)(2,1)S(1)}, bf16[2,128,1536]{2,1,0:T(8,128)(2,1)S(1)}, u32[]{:S(2)}, u32[]{:S(2)}) %collective-permute-start) | collective-permute-done | bytes 786464 | tf_op jit(solution)/shard_map/ppermute | solution.py:447
  81.3 0.9 copy-done.4
  82.2 11.9 %qkv.2 = (bf16[2,8,3,128,128]{4,3,2,1,0:T(8,128)(2,1)}, bf16[2,6,2,128,128]{4,3,2,1,0:T(8,128)(2,1)}) custom-call(s32[2]{0:T(128)} %pad_add_fusion.info, bf16[2,256,1536]{2,1,0:T(8,128)(2,1)} %hidden.1, bf16[2,128,1536]{2,1,0:T(8,128)(2,1)} %copy-done.4, f32[3,2,3072]{2,1,0:T(2,128)} %bitcast.43, f32[3,2,3072]{2,1,0:T(2,128)} %bitcast.44, ...), custom_call_target="tpu_custom_call" | custom-call | flops 3623878656 | bytes 20000000 | tf_op jit(solution)/shard_map/qkv/pallas_call | solution.py:125
  94.1 4.7 %all-to-all-start = ((bf16[16,3,128,128]{3,2,1,0:T(8,128)(2,1)}), bf16[16,3,128,128]{3,2,1,0:T(8,128)(2,1)}, u32[]{:S(2)}, u32[]{:S(2)}) async-start(bf16[16,3,128,128]{3,2,1,0:T(8,128)(2,1)} %bitcast.39), calls=%async_computation | async-start | bytes 3145728 | tf_op jit(solution)/shard_map/all_to_all | solution.py:495
  98.8 0.7 fusion.15
  99.4 0.8 copy.21
  100.2 1.9 collective-permute-start.4
  102.1 2.7 %collective-permute-start.5 = (bf16[48,1536]{1,0:T(8,128)(2,1)S(1)}, bf16[48,1536]{1,0:T(8,128)(2,1)S(1)}, u32[]{:S(2)}, u32[]{:S(2)}) collective-permute-start(bf16[48,1536]{1,0:T(8,128)(2,1)S(1)} %collective-permute-done.3), channel_id=1, source_target_pairs={{0,16},{2,18},{4,20},{6,22},{8,24},{10,26},{12,28},{14,30},{16,0},... | collective-permute-start | bytes 442376 | tf_op jit(solution)/shard_map/ppermute | solution.py:503
  104.8 1.5 collective-permute-start.6
  106.3 5.9 %diag.1.near = bf16[2,6,144,256]{3,2,1,0:T(8,128)(2,1)} custom-call(bf16[2,8,3,128,128]{4,3,2,1,0:T(8,128)(2,1)} %get-tuple-element.13.refs_0_, bf16[2,8,3,128,128]{4,3,2,1,0:T(8,128)(2,1)} %get-tuple-element.14.refs_1_, bf16[2,6,2,128,128]{4,3,2,1,0:T(8,128)(2,1)} %get-tuple-element.15.refs_2_, bf16[2,6,2,128,128]{4,3,2,1,0:T(8,128)(2,1)} %get-tuple-element.16.refs_3_), custom_call_target="tpu_custom_call" | custom-call | flops 402653184 | bytes 4000000 | tf_op jit(solution)/shard_map/diag/pallas_call | solution.py:200
  112.2 11.1 %collective-permute-done.4 = bf16[48,1536]{1,0:T(8,128)(2,1)S(1)} collective-permute-done((bf16[48,1536]{1,0:T(8,128)(2,1)S(1)}, bf16[48,1536]{1,0:T(8,128)(2,1)S(1)}, u32[]{:S(2)}, u32[]{:S(2)}) %collective-permute-start.4) | collective-permute-done | bytes 147488 | tf_op jit(solution)/shard_map/ppermute | solution.py:503
  123.3 3.2 %collective-permute-done.5 = bf16[48,1536]{1,0:T(8,128)(2,1)S(1)} collective-permute-done((bf16[48,1536]{1,0:T(8,128)(2,1)S(1)}, bf16[48,1536]{1,0:T(8,128)(2,1)S(1)}, u32[]{:S(2)}, u32[]{:S(2)}) %collective-permute-start.5) | collective-permute-done | bytes 147488 | tf_op jit(solution)/shard_map/ppermute | solution.py:503
  126.5 26.3 %attend.1 = bf16[16,2,144,256]{3,2,1,0:T(8,128)(2,1)} custom-call(s32[1]{0:T(128)} %bitcast.2.info, bf16[16,3,128,128]{3,2,1,0:T(8,128)(2,1)} %all-to-all-done.got_0, bf16[16,3,128,128]{3,2,1,0:T(8,128)(2,1)} %copy-done.3, bf16[512,128]{1,0:T(8,128)(2,1)} %bitcast.47, bf16[128,512]{1,0:T(8,128)(2,1)} %bitcast.46), custom_call_target="tpu_custom_call" | custom-call | flops 18253611008 | bytes 8000000 | tf_op jit(solution)/shard_map/attend/pallas_call | solution.py:317
  152.8 4.1 %all-to-all-start.3 = ((bf16[32,144,256]{2,1,0:T(8,128)(2,1)}), bf16[32,144,256]{2,1,0:T(8,128)(2,1)S(1)}, u32[]{:S(2)}, u32[]{:S(2)}) async-start(bf16[32,144,256]{2,1,0:T(8,128)(2,1)} %bitcast.40), calls=%async_computation.3 | async-start | bytes 4718592 | tf_op jit(solution)/shard_map/all_to_all | solution.py:518
  156.9 2.0 collective-permute-start.7
  159.0 0.7 constant_dynamic-slice_fusion
  159.7 0.6 copy.23.gate
  160.3 3.6 %collective-permute-start.8 = (bf16[4,48,1536]{2,1,0:T(8,128)(2,1)S(1)}, bf16[4,48,1536]{2,1,0:T(8,128)(2,1)S(1)}, u32[]{:S(2)}, u32[]{:S(2)}) collective-permute-start(bf16[4,48,1536]{2,1,0:T(8,128)(2,1)S(1)} %bitcast_dynamic-update-slice_fusion.4), channel_id=1, source_target_pairs={{0,64},{32,96},{64,0},{96,32},{1,65},{33,97},{65,1},{97,33},{2,66}... | collective-permute-start | bytes 1769480 | tf_op jit(solution)/shard_map/ppermute | solution.py:509
  163.9 1.0 collective-permute-start.9
  164.9 0.2 broadcast_in_dim.81
  165.2 9.6 %collective-permute-done.7 = bf16[4,48,1536]{2,1,0:T(8,128)(2,1)S(1)} collective-permute-done((bf16[4,48,1536]{2,1,0:T(8,128)(2,1)S(1)}, bf16[4,48,1536]{2,1,0:T(8,128)(2,1)S(1)}, u32[]{:S(2)}, u32[]{:S(2)}) %collective-permute-start.7) | collective-permute-done | bytes 589856 | tf_op jit(solution)/shard_map/ppermute | solution.py:509
  174.8 3.2 %collective-permute-start.2 = (bf16[2,6,144,256]{3,2,1,0:T(8,128)(2,1)S(1)}, bf16[2,6,144,256]{3,2,1,0:T(8,128)(2,1)}, u32[]{:S(2)}, u32[]{:S(2)}) collective-permute-start(bf16[2,6,144,256]{3,2,1,0:T(8,128)(2,1)S(1)} %copy-done.2), channel_id=1, source_target_pairs={{0,1},{1,0},{2,3},{3,2},{4,5},{5,4},{6,7},{7,6},{8,9},{9,8},{10,11... | collective-permute-start | bytes 2654216 | tf_op jit(solution)/shard_map/ppermute | solution.py:514
  178.0 10.5 %collective-permute-done.8 = bf16[4,48,1536]{2,1,0:T(8,128)(2,1)S(1)} collective-permute-done((bf16[4,48,1536]{2,1,0:T(8,128)(2,1)S(1)}, bf16[4,48,1536]{2,1,0:T(8,128)(2,1)S(1)}, u32[]{:S(2)}, u32[]{:S(2)}) %collective-permute-start.8) | collective-permute-done | bytes 589856 | tf_op jit(solution)/shard_map/ppermute | solution.py:509
  188.6 0.7 collective-permute-done.9
  189.4 1.4 copy-done.1
  190.8 16.1 %collective-permute-done.2.far = bf16[2,6,144,256]{3,2,1,0:T(8,128)(2,1)} collective-permute-done((bf16[2,6,144,256]{3,2,1,0:T(8,128)(2,1)S(1)}, bf16[2,6,144,256]{3,2,1,0:T(8,128)(2,1)}, u32[]{:S(2)}, u32[]{:S(2)}) %collective-permute-start.2) | collective-permute-done | bytes 884768 | tf_op jit(solution)/shard_map/ppermute | solution.py:514
  207.0 1.4 copy-done
  208.4 9.8 %project.1 = bf16[2,256,1536]{2,1,0:T(8,128)(2,1)} custom-call(s32[2]{0:T(128)} %pad_add_fusion.info, bf16[32,144,256]{2,1,0:T(8,128)(2,1)} %copy-done, bf16[2,6,144,256]{3,2,1,0:T(8,128)(2,1)} %diag.1.near, bf16[2,6,144,256]{3,2,1,0:T(8,128)(2,1)} %collective-permute-done.2.far, bf16[768,3072]{1,0:T(8,128)(2,1)} %w_own.1, bf16[768,1536]{1,0:T(8,128)(2,1)} %bitcast.37, ...), custom_call_target="tpu_custom_call" | custom-call | flops 2415919104 | bytes 12000000 | tf_op jit(solution)/shard_map/project/pallas_call | solution.py:387
  (42 shorter events, 0.7 us)
Async XLA Ops:
  0.0 4.8 %copy-start.6 = (bf16[2,32,768]{2,1,0:T(8,128)(2,1)S(1)}, bf16[2,32,768]{2,1,0:T(8,128)(2,1)}, u32[]{:S(2)}) copy-start(bf16[2,32,768]{2,1,0:T(8,128)(2,1)} %param.21) | copy-start | bytes 294916
  0.0 5.0 %copy-start.7 = (bf16[2,32,768]{2,1,0:T(8,128)(2,1)S(1)}, bf16[2,32,768]{2,1,0:T(8,128)(2,1)}, u32[]{:S(2)}) copy-start(bf16[2,32,768]{2,1,0:T(8,128)(2,1)} %param.20) | copy-start | bytes 294916
  0.0 10.6 %copy-start.10 = (s32[16]{0:T(128)S(1)}, s32[16]{0:T(128)}, u32[]{:S(2)}) copy-start(s32[16]{0:T(128)} %param.26) | copy-start | bytes 196
  0.0 11.3 %copy-start.11 = (s32[16]{0:T(128)S(1)}, s32[16]{0:T(128)}, u32[]{:S(2)}) copy-start(s32[16]{0:T(128)} %param.25) | copy-start | bytes 196
  0.0 13.9 %copy-start.8 = (f32[128]{0:T(128)S(1)}, f32[128]{0:T(128)}, u32[]{:S(2)}) copy-start(f32[128]{0:T(128)} %param.19) | copy-start | bytes 1540
  0.0 13.9 %copy-start.9 = (f32[128]{0:T(128)S(1)}, f32[128]{0:T(128)}, u32[]{:S(2)}) copy-start(f32[128]{0:T(128)} %param.18) | copy-start | bytes 1540
  1.6 22.0 %collective-permute-start.1 = (bf16[2,128,1536]{2,1,0:T(8,128)(2,1)S(1)}, bf16[2,128,1536]{2,1,0:T(8,128)(2,1)S(1)}, u32[]{:S(2)}, u32[]{:S(2)}) collective-permute-start(bf16[2,128,1536]{2,1,0:T(8,128)(2,1)S(1)} %get-tuple-element.21), channel_id=1, source_target_pairs={{0,1},{1,0},{2,3},{3,2},{4,5},{5,4},{6,7},{7,6},{8,9},{9,8},{10,11... | collective-permute-start | bytes 2359304 | tf_op jit(solution)/shard_map/ppermute | solution.py:447
  6.0 30.4 %all-to-all-start.2 = ((bf16[16,2,32,128]{3,2,1,0:T(8,128)(2,1)}), bf16[16,2,32,128]{3,2,1,0:T(8,128)(2,1)S(1)}, u32[]{:S(2)}, u32[]{:S(2)}) async-start(bf16[16,2,32,128]{3,2,1,0:T(8,128)(2,1)} %bitcast.10), calls=%async_computation.2 | async-start | bytes 524288 | tf_op jit(solution)/shard_map/all_to_all | solution.py:454
  23.6 0.9 copy-start.5
  36.3 57.7 %all-to-all-start.1 = ((bf16[16,3,128,128]{3,2,1,0:T(8,128)(2,1)}), bf16[16,3,128,128]{3,2,1,0:T(8,128)(2,1)S(1)}, u32[]{:S(2)}, u32[]{:S(2)}) async-start(bf16[16,3,128,128]{3,2,1,0:T(8,128)(2,1)} %bitcast.38), calls=%async_computation.1 | async-start | bytes 3145728 | tf_op jit(solution)/shard_map/all_to_all | solution.py:495
  42.0 39.2 %collective-permute-start = (bf16[2,128,1536]{2,1,0:T(8,128)(2,1)S(1)}, bf16[2,128,1536]{2,1,0:T(8,128)(2,1)S(1)}, u32[]{:S(2)}, u32[]{:S(2)}) collective-permute-start(bf16[2,128,1536]{2,1,0:T(8,128)(2,1)S(1)} %get-tuple-element.22), channel_id=1, source_target_pairs={{0,1},{1,0},{2,3},{3,2},{4,5},{5,4},{6,7},{7,6},{8,9},{9,8},{10,11... | collective-permute-start | bytes 2359304 | tf_op jit(solution)/shard_map/ppermute | solution.py:447
  46.4 53.8 %collective-permute-start.3 = (bf16[48,1536]{1,0:T(8,128)(2,1)}, bf16[48,1536]{1,0:T(8,128)(2,1)S(1)}, u32[]{:S(2)}, u32[]{:S(2)}) collective-permute-start(bf16[48,1536]{1,0:T(8,128)(2,1)} %dynamic_slice.6), channel_id=1, source_target_pairs={{0,1},{1,0},{2,3},{3,2},{4,5},{5,4},{6,7},{7,6},{8,9},{9,8},{10,11... | collective-permute-start | bytes 442376 | tf_op jit(solution)/shard_map/ppermute | solution.py:466
  81.3 0.9 copy-start.4
  94.1 12.2 %copy-start.3 = (bf16[16,3,128,128]{3,2,1,0:T(8,128)(2,1)}, bf16[16,3,128,128]{3,2,1,0:T(8,128)(2,1)S(1)}, u32[]{:S(2)}) copy-start(bf16[16,3,128,128]{3,2,1,0:T(8,128)(2,1)S(1)} %all-to-all-done.1.got_1) | copy-start | bytes 4718596
  94.1 32.4 %all-to-all-start = ((bf16[16,3,128,128]{3,2,1,0:T(8,128)(2,1)}), bf16[16,3,128,128]{3,2,1,0:T(8,128)(2,1)}, u32[]{:S(2)}, u32[]{:S(2)}) async-start(bf16[16,3,128,128]{3,2,1,0:T(8,128)(2,1)} %bitcast.39), calls=%async_computation | async-start | bytes 3145728 | tf_op jit(solution)/shard_map/all_to_all | solution.py:495
  100.2 23.1 %collective-permute-start.4 = (bf16[48,1536]{1,0:T(8,128)(2,1)S(1)}, bf16[48,1536]{1,0:T(8,128)(2,1)S(1)}, u32[]{:S(2)}, u32[]{:S(2)}) collective-permute-start(bf16[48,1536]{1,0:T(8,128)(2,1)S(1)} %collective-permute-done.3), channel_id=1, source_target_pairs={{0,8},{2,10},{4,12},{6,14},{8,16},{10,18},{12,20},{14,22},{16,24},... | collective-permute-start | bytes 442376 | tf_op jit(solution)/shard_map/ppermute | solution.py:503
  102.1 24.4 %collective-permute-start.5 = (bf16[48,1536]{1,0:T(8,128)(2,1)S(1)}, bf16[48,1536]{1,0:T(8,128)(2,1)S(1)}, u32[]{:S(2)}, u32[]{:S(2)}) collective-permute-start(bf16[48,1536]{1,0:T(8,128)(2,1)S(1)} %collective-permute-done.3), channel_id=1, source_target_pairs={{0,16},{2,18},{4,20},{6,22},{8,24},{10,26},{12,28},{14,30},{16,0},... | collective-permute-start | bytes 442376 | tf_op jit(solution)/shard_map/ppermute | solution.py:503
  104.8 52.1 %collective-permute-start.6 = (bf16[48,1536]{1,0:T(8,128)(2,1)S(1)}, bf16[48,1536]{1,0:T(8,128)(2,1)S(1)}, u32[]{:S(2)}, u32[]{:S(2)}) collective-permute-start(bf16[48,1536]{1,0:T(8,128)(2,1)S(1)} %collective-permute-done.3), channel_id=1, source_target_pairs={{0,24},{2,26},{4,28},{6,30},{8,0},{10,2},{12,4},{14,6},{16,8},{18,... | collective-permute-start | bytes 442376 | tf_op jit(solution)/shard_map/ppermute | solution.py:503
  152.8 54.1 %all-to-all-start.3 = ((bf16[32,144,256]{2,1,0:T(8,128)(2,1)}), bf16[32,144,256]{2,1,0:T(8,128)(2,1)S(1)}, u32[]{:S(2)}, u32[]{:S(2)}) async-start(bf16[32,144,256]{2,1,0:T(8,128)(2,1)} %bitcast.40), calls=%async_computation.3 | async-start | bytes 4718592 | tf_op jit(solution)/shard_map/all_to_all | solution.py:518
  156.9 17.8 %collective-permute-start.7 = (bf16[4,48,1536]{2,1,0:T(8,128)(2,1)S(1)}, bf16[4,48,1536]{2,1,0:T(8,128)(2,1)S(1)}, u32[]{:S(2)}, u32[]{:S(2)}) collective-permute-start(bf16[4,48,1536]{2,1,0:T(8,128)(2,1)S(1)} %bitcast_dynamic-update-slice_fusion.4), channel_id=1, source_target_pairs={{0,32},{32,64},{64,96},{96,0},{1,33},{33,65},{65,97},{97,1},{2,34}... | collective-permute-start | bytes 1769480 | tf_op jit(solution)/shard_map/ppermute | solution.py:509
  160.3 14.5 %copy-start.2 = (bf16[2,6,144,256]{3,2,1,0:T(8,128)(2,1)S(1)}, bf16[2,6,144,256]{3,2,1,0:T(8,128)(2,1)}, u32[]{:S(2)}) copy-start(bf16[2,6,144,256]{3,2,1,0:T(8,128)(2,1)} %diag.1.near) | copy-start | bytes 2654212
  160.3 28.3 %collective-permute-start.8 = (bf16[4,48,1536]{2,1,0:T(8,128)(2,1)S(1)}, bf16[4,48,1536]{2,1,0:T(8,128)(2,1)S(1)}, u32[]{:S(2)}, u32[]{:S(2)}) collective-permute-start(bf16[4,48,1536]{2,1,0:T(8,128)(2,1)S(1)} %bitcast_dynamic-update-slice_fusion.4), channel_id=1, source_target_pairs={{0,64},{32,96},{64,0},{96,32},{1,65},{33,97},{65,1},{97,33},{2,66}... | collective-permute-start | bytes 1769480 | tf_op jit(solution)/shard_map/ppermute | solution.py:509
  163.9 25.5 %collective-permute-start.9 = (bf16[4,48,1536]{2,1,0:T(8,128)(2,1)S(1)}, bf16[4,48,1536]{2,1,0:T(8,128)(2,1)S(1)}, u32[]{:S(2)}, u32[]{:S(2)}) collective-permute-start(bf16[4,48,1536]{2,1,0:T(8,128)(2,1)S(1)} %bitcast_dynamic-update-slice_fusion.4), channel_id=1, source_target_pairs={{0,96},{32,0},{64,32},{96,64},{1,97},{33,1},{65,33},{97,65},{2,98}... | collective-permute-start | bytes 1769480 | tf_op jit(solution)/shard_map/ppermute | solution.py:509
  174.8 32.1 %collective-permute-start.2 = (bf16[2,6,144,256]{3,2,1,0:T(8,128)(2,1)S(1)}, bf16[2,6,144,256]{3,2,1,0:T(8,128)(2,1)}, u32[]{:S(2)}, u32[]{:S(2)}) collective-permute-start(bf16[2,6,144,256]{3,2,1,0:T(8,128)(2,1)S(1)} %copy-done.2), channel_id=1, source_target_pairs={{0,1},{1,0},{2,3},{3,2},{4,5},{5,4},{6,7},{7,6},{8,9},{9,8},{10,11... | collective-permute-start | bytes 2654216 | tf_op jit(solution)/shard_map/ppermute | solution.py:514
  189.4 1.4 copy-start.1
  207.0 1.4 copy-start

commit v2 on v1

--- a/solution.py
+++ b/solution.py
@@ -368,7 +368,9 @@
                     b = log_sum(own[p, j, 128:144, :])
                     high = jnp.maximum(a, b)
                     a, b = jnp.exp2(a - high), jnp.exp2(b - high)
-                    o = (got[at, 0:128, :].astype(F32) * a + own[p, j, 0:128, :].astype(F32) * b) / (a + b)
+                    shrink = 1.0 / (a + b)
+                    a, b = a * shrink, b * shrink
+                    o = got[at, 0:128, :].astype(F32) * a + own[p, j, 0:128, :].astype(F32) * b
                     col = (k * heads + j) * 128
                     all_s[p * rows : (p + 1) * rows, col : col + 128] = jnp.transpose(o.astype(BF16))
 
@@ -382,7 +384,7 @@
 def project(info, got, near, far, w_out, w_oth, gate, hidden, cached):
     prompts, rows, width = hidden.shape
     part = w_out.shape[0]
-    bn = 512
+    bn = 768
     steps = width // bn
     return pl.pallas_call(
         project_body,

time: 219 us -> 219 us (level)
  no operation moved by 1% of the time
where the time goes in v2:
time: 219 us; the launch traced here: 218 us
  waiting for transfers between devices  89.7 us (41%)
  Pallas kernels  65.4 us (30%)
  starting transfers between devices  41.8 us (19%)
  local copies, waits for them, and re-layouts  13.4 us (6%)
  other arithmetic  6.65 us (3%)
    ppermute x2, waiting for transfers between devices, per_device(): lax.ppermute(image_hidden[:, i * half:(i + 1) * half], 'head', swap)  38.4 us
    pallas_call x1, Pallas kernels, attend(): pl.pallas_call(attend_body, grid_spec=pltpu.PrefetchScalarGridSpec(num_sc...  26.3 us
    pallas_call x2, Pallas kernels, qkv(): pl.pallas_call(qkv_body, grid_spec=pltpu.PrefetchScalarGridSpec(num_scala...  23.8 us
    ppermute x3, waiting for transfers between devices, per_device(): lax.ppermute(w_y, 'batch', [(i, (i + d) % n_batch) for i in range(n_batch)])  20.9 us
    ppermute x1, waiting for transfers between devices, per_device(): far = lax.ppermute(near_sent, 'head', swap)  16.1 us
    ppermute x3, waiting for transfers between devices, per_device(): lax.ppermute(piece, 'seq', [(i, (i + 4 * d) % n_seq) for i in range(n_seq)])  14.3 us
    all_to_all x2, starting transfers between devices, per_device(): lax.all_to_all(s.reshape(n_seq, 3, half, head_dim), 'seq', split_axis=0,...  10.4 us
    pallas_call x1, Pallas kernels, project(): pl.pallas_call(project_body, grid_spec=pltpu.PrefetchScalarGridSpec(num_s...  9.46 us
  transfers between devices with their start and end apart: 14, of which 8 were waited for; matrix products, arithmetic and copies ran while one was open for 6% of the time, Pallas kernels for 26%

profile of v2, /device:TPU:0, one launch (start us, length us, event | category | flops | bytes accessed | tf_op | source)
XLA Modules:
  0.0 217.9 jit_solution(6852081565553589592)
XLA Ops:
  0.0 1.5 fusion.14
  1.6 3.3 %collective-permute-start.1 = (bf16[2,128,1536]{2,1,0:T(8,128)(2,1)S(1)}, bf16[2,128,1536]{2,1,0:T(8,128)(2,1)S(1)}, u32[]{:S(2)}, u32[]{:S(2)}) collective-permute-start(bf16[2,128,1536]{2,1,0:T(8,128)(2,1)S(1)} %get-tuple-element.21), channel_id=1, source_target_pairs={{0,1},{1,0},{2,3},{3,2},{4,5},{5,4},{6,7},{7,6},{8,9},{9,8},{10,11... | collective-permute-start | bytes 2359304 | tf_op jit(solution)/shard_map/ppermute | solution.py:449
  5.2 0.7 pad.4.clone
  6.0 4.6 %all-to-all-start.2 = ((bf16[16,2,32,128]{3,2,1,0:T(8,128)(2,1)}), bf16[16,2,32,128]{3,2,1,0:T(8,128)(2,1)S(1)}, u32[]{:S(2)}, u32[]{:S(2)}) async-start(bf16[16,2,32,128]{3,2,1,0:T(8,128)(2,1)} %bitcast.10), calls=%async_computation.2 | async-start | bytes 524288 | tf_op jit(solution)/shard_map/all_to_all | solution.py:456
  10.6 0.6 fusion.11
  11.3 0.7 fusion.12
  12.6 1.3 pad_add_fusion.info
  13.9 0.5 pad_maximum_fusion.2.gains
  14.5 0.5 fusion.2
  15.1 0.8 pad_maximum_fusion.cos
  15.8 0.8 pad_maximum_fusion.1.sin
  16.6 7.0 %collective-permute-done.1.oth = bf16[2,128,1536]{2,1,0:T(8,128)(2,1)S(1)} collective-permute-done((bf16[2,128,1536]{2,1,0:T(8,128)(2,1)S(1)}, bf16[2,128,1536]{2,1,0:T(8,128)(2,1)S(1)}, u32[]{:S(2)}, u32[]{:S(2)}) %collective-permute-start.1) | collective-permute-done | bytes 786464 | tf_op jit(solution)/shard_map/ppermute | solution.py:449
  23.6 0.9 copy-done.5
  24.4 11.9 %qkv.3 = (bf16[2,8,3,128,128]{4,3,2,1,0:T(8,128)(2,1)}, bf16[2,6,2,128,128]{4,3,2,1,0:T(8,128)(2,1)}) custom-call(s32[2]{0:T(128)} %pad_add_fusion.info, bf16[2,256,1536]{2,1,0:T(8,128)(2,1)} %hidden.1, bf16[2,128,1536]{2,1,0:T(8,128)(2,1)} %copy-done.5, f32[3,2,3072]{2,1,0:T(2,128)} %bitcast.41, f32[3,2,3072]{2,1,0:T(2,128)} %bitcast.42, ...), custom_call_target="tpu_custom_call" | custom-call | flops 3623878656 | bytes 20000000 | tf_op jit(solution)/shard_map/qkv/pallas_call | solution.py:125
  36.3 5.7 %all-to-all-start.1 = ((bf16[16,3,128,128]{3,2,1,0:T(8,128)(2,1)}), bf16[16,3,128,128]{3,2,1,0:T(8,128)(2,1)S(1)}, u32[]{:S(2)}, u32[]{:S(2)}) async-start(bf16[16,3,128,128]{3,2,1,0:T(8,128)(2,1)} %bitcast.38), calls=%async_computation.1 | async-start | bytes 3145728 | tf_op jit(solution)/shard_map/all_to_all | solution.py:497
  42.0 2.8 %collective-permute-start = (bf16[2,128,1536]{2,1,0:T(8,128)(2,1)S(1)}, bf16[2,128,1536]{2,1,0:T(8,128)(2,1)S(1)}, u32[]{:S(2)}, u32[]{:S(2)}) collective-permute-start(bf16[2,128,1536]{2,1,0:T(8,128)(2,1)S(1)} %get-tuple-element.22), channel_id=1, source_target_pairs={{0,1},{1,0},{2,3},{3,2},{4,5},{5,4},{6,7},{7,6},{8,9},{9,8},{10,11... | collective-permute-start | bytes 2359304 | tf_op jit(solution)/shard_map/ppermute | solution.py:449
  44.8 1.6 dynamic_slice.6
  46.4 0.8 collective-permute-start.3
  47.2 1.3 slice.19
  48.6 1.3 fusion.13
  49.9 31.4 %collective-permute-done.oth = bf16[2,128,1536]{2,1,0:T(8,128)(2,1)S(1)} collective-permute-done((bf16[2,128,1536]{2,1,0:T(8,128)(2,1)S(1)}, bf16[2,128,1536]{2,1,0:T(8,128)(2,1)S(1)}, u32[]{:S(2)}, u32[]{:S(2)}) %collective-permute-start) | collective-permute-done | bytes 786464 | tf_op jit(solution)/shard_map/ppermute | solution.py:449
  81.3 0.9 copy-done.4
  82.2 11.9 %qkv.2 = (bf16[2,8,3,128,128]{4,3,2,1,0:T(8,128)(2,1)}, bf16[2,6,2,128,128]{4,3,2,1,0:T(8,128)(2,1)}) custom-call(s32[2]{0:T(128)} %pad_add_fusion.info, bf16[2,256,1536]{2,1,0:T(8,128)(2,1)} %hidden.1, bf16[2,128,1536]{2,1,0:T(8,128)(2,1)} %copy-done.4, f32[3,2,3072]{2,1,0:T(2,128)} %bitcast.43, f32[3,2,3072]{2,1,0:T(2,128)} %bitcast.44, ...), custom_call_target="tpu_custom_call" | custom-call | flops 3623878656 | bytes 20000000 | tf_op jit(solution)/shard_map/qkv/pallas_call | solution.py:125
  94.1 4.7 %all-to-all-start = ((bf16[16,3,128,128]{3,2,1,0:T(8,128)(2,1)}), bf16[16,3,128,128]{3,2,1,0:T(8,128)(2,1)}, u32[]{:S(2)}, u32[]{:S(2)}) async-start(bf16[16,3,128,128]{3,2,1,0:T(8,128)(2,1)} %bitcast.39), calls=%async_computation | async-start | bytes 3145728 | tf_op jit(solution)/shard_map/all_to_all | solution.py:497
  98.8 0.7 fusion.15
  99.4 0.8 copy.21
  100.2 1.9 collective-permute-start.4
  102.1 2.7 %collective-permute-start.5 = (bf16[48,1536]{1,0:T(8,128)(2,1)S(1)}, bf16[48,1536]{1,0:T(8,128)(2,1)S(1)}, u32[]{:S(2)}, u32[]{:S(2)}) collective-permute-start(bf16[48,1536]{1,0:T(8,128)(2,1)S(1)} %collective-permute-done.3), channel_id=1, source_target_pairs={{0,16},{2,18},{4,20},{6,22},{8,24},{10,26},{12,28},{14,30},{16,0},... | collective-permute-start | bytes 442376 | tf_op jit(solution)/shard_map/ppermute | solution.py:505
  104.8 1.5 collective-permute-start.6
  106.3 5.9 %diag.1.near = bf16[2,6,144,256]{3,2,1,0:T(8,128)(2,1)} custom-call(bf16[2,8,3,128,128]{4,3,2,1,0:T(8,128)(2,1)} %get-tuple-element.13.refs_0_, bf16[2,8,3,128,128]{4,3,2,1,0:T(8,128)(2,1)} %get-tuple-element.14.refs_1_, bf16[2,6,2,128,128]{4,3,2,1,0:T(8,128)(2,1)} %get-tuple-element.15.refs_2_, bf16[2,6,2,128,128]{4,3,2,1,0:T(8,128)(2,1)} %get-tuple-element.16.refs_3_), custom_call_target="tpu_custom_call" | custom-call | flops 402653184 | bytes 4000000 | tf_op jit(solution)/shard_map/diag/pallas_call | solution.py:200
  112.2 11.1 %collective-permute-done.4 = bf16[48,1536]{1,0:T(8,128)(2,1)S(1)} collective-permute-done((bf16[48,1536]{1,0:T(8,128)(2,1)S(1)}, bf16[48,1536]{1,0:T(8,128)(2,1)S(1)}, u32[]{:S(2)}, u32[]{:S(2)}) %collective-permute-start.4) | collective-permute-done | bytes 147488 | tf_op jit(solution)/shard_map/ppermute | solution.py:505
  123.3 3.2 %collective-permute-done.5 = bf16[48,1536]{1,0:T(8,128)(2,1)S(1)} collective-permute-done((bf16[48,1536]{1,0:T(8,128)(2,1)S(1)}, bf16[48,1536]{1,0:T(8,128)(2,1)S(1)}, u32[]{:S(2)}, u32[]{:S(2)}) %collective-permute-start.5) | collective-permute-done | bytes 147488 | tf_op jit(solution)/shard_map/ppermute | solution.py:505
  126.5 26.3 %attend.1 = bf16[16,2,144,256]{3,2,1,0:T(8,128)(2,1)} custom-call(s32[1]{0:T(128)} %bitcast.2.info, bf16[16,3,128,128]{3,2,1,0:T(8,128)(2,1)} %all-to-all-done.got_0, bf16[16,3,128,128]{3,2,1,0:T(8,128)(2,1)} %copy-done.3, bf16[512,128]{1,0:T(8,128)(2,1)} %bitcast.47, bf16[128,512]{1,0:T(8,128)(2,1)} %bitcast.46), custom_call_target="tpu_custom_call" | custom-call | flops 18253611008 | bytes 8000000 | tf_op jit(solution)/shard_map/attend/pallas_call | solution.py:317
  152.8 4.1 %all-to-all-start.3 = ((bf16[32,144,256]{2,1,0:T(8,128)(2,1)}), bf16[32,144,256]{2,1,0:T(8,128)(2,1)S(1)}, u32[]{:S(2)}, u32[]{:S(2)}) async-start(bf16[32,144,256]{2,1,0:T(8,128)(2,1)} %bitcast.40), calls=%async_computation.3 | async-start | bytes 4718592 | tf_op jit(solution)/shard_map/all_to_all | solution.py:520
  156.9 2.0 collective-permute-start.7
  159.0 0.7 constant_dynamic-slice_fusion
  159.7 0.6 copy.23.gate
  160.3 3.6 %collective-permute-start.8 = (bf16[4,48,1536]{2,1,0:T(8,128)(2,1)S(1)}, bf16[4,48,1536]{2,1,0:T(8,128)(2,1)S(1)}, u32[]{:S(2)}, u32[]{:S(2)}) collective-permute-start(bf16[4,48,1536]{2,1,0:T(8,128)(2,1)S(1)} %bitcast_dynamic-update-slice_fusion.4), channel_id=1, source_target_pairs={{0,64},{32,96},{64,0},{96,32},{1,65},{33,97},{65,1},{97,33},{2,66}... | collective-permute-start | bytes 1769480 | tf_op jit(solution)/shard_map/ppermute | solution.py:511
  163.9 1.0 collective-permute-start.9
  164.9 0.2 broadcast_in_dim.81
  165.2 9.6 %collective-permute-done.7 = bf16[4,48,1536]{2,1,0:T(8,128)(2,1)S(1)} collective-permute-done((bf16[4,48,1536]{2,1,0:T(8,128)(2,1)S(1)}, bf16[4,48,1536]{2,1,0:T(8,128)(2,1)S(1)}, u32[]{:S(2)}, u32[]{:S(2)}) %collective-permute-start.7) | collective-permute-done | bytes 589856 | tf_op jit(solution)/shard_map/ppermute | solution.py:511
  174.8 3.2 %collective-permute-start.2 = (bf16[2,6,144,256]{3,2,1,0:T(8,128)(2,1)S(1)}, bf16[2,6,144,256]{3,2,1,0:T(8,128)(2,1)}, u32[]{:S(2)}, u32[]{:S(2)}) collective-permute-start(bf16[2,6,144,256]{3,2,1,0:T(8,128)(2,1)S(1)} %copy-done.2), channel_id=1, source_target_pairs={{0,1},{1,0},{2,3},{3,2},{4,5},{5,4},{6,7},{7,6},{8,9},{9,8},{10,11... | collective-permute-start | bytes 2654216 | tf_op jit(solution)/shard_map/ppermute | solution.py:516
  178.0 10.5 %collective-permute-done.8 = bf16[4,48,1536]{2,1,0:T(8,128)(2,1)S(1)} collective-permute-done((bf16[4,48,1536]{2,1,0:T(8,128)(2,1)S(1)}, bf16[4,48,1536]{2,1,0:T(8,128)(2,1)S(1)}, u32[]{:S(2)}, u32[]{:S(2)}) %collective-permute-start.8) | collective-permute-done | bytes 589856 | tf_op jit(solution)/shard_map/ppermute | solution.py:511
  188.6 0.7 collective-permute-done.9
  189.4 1.4 copy-done.1
  190.8 16.1 %collective-permute-done.2.far = bf16[2,6,144,256]{3,2,1,0:T(8,128)(2,1)} collective-permute-done((bf16[2,6,144,256]{3,2,1,0:T(8,128)(2,1)S(1)}, bf16[2,6,144,256]{3,2,1,0:T(8,128)(2,1)}, u32[]{:S(2)}, u32[]{:S(2)}) %collective-permute-start.2) | collective-permute-done | bytes 884768 | tf_op jit(solution)/shard_map/ppermute | solution.py:516
  207.0 1.4 copy-done
  208.4 9.5 %project.1 = bf16[2,256,1536]{2,1,0:T(8,128)(2,1)} custom-call(s32[2]{0:T(128)} %pad_add_fusion.info, bf16[32,144,256]{2,1,0:T(8,128)(2,1)} %copy-done, bf16[2,6,144,256]{3,2,1,0:T(8,128)(2,1)} %diag.1.near, bf16[2,6,144,256]{3,2,1,0:T(8,128)(2,1)} %collective-permute-done.2.far, bf16[768,3072]{1,0:T(8,128)(2,1)} %w_own.1, bf16[768,1536]{1,0:T(8,128)(2,1)} %bitcast.37, ...), custom_call_target="tpu_custom_call" | custom-call | flops 2415919104 | bytes 12000000 | tf_op jit(solution)/shard_map/project/pallas_call | solution.py:389
  (42 shorter events, 0.7 us)
Async XLA Ops:
  0.0 4.8 %copy-start.6 = (bf16[2,32,768]{2,1,0:T(8,128)(2,1)S(1)}, bf16[2,32,768]{2,1,0:T(8,128)(2,1)}, u32[]{:S(2)}) copy-start(bf16[2,32,768]{2,1,0:T(8,128)(2,1)} %param.21) | copy-start | bytes 294916
  0.0 5.0 %copy-start.7 = (bf16[2,32,768]{2,1,0:T(8,128)(2,1)S(1)}, bf16[2,32,768]{2,1,0:T(8,128)(2,1)}, u32[]{:S(2)}) copy-start(bf16[2,32,768]{2,1,0:T(8,128)(2,1)} %param.20) | copy-start | bytes 294916
  0.0 10.6 %copy-start.10 = (s32[16]{0:T(128)S(1)}, s32[16]{0:T(128)}, u32[]{:S(2)}) copy-start(s32[16]{0:T(128)} %param.26) | copy-start | bytes 196
  0.0 11.3 %copy-start.11 = (s32[16]{0:T(128)S(1)}, s32[16]{0:T(128)}, u32[]{:S(2)}) copy-start(s32[16]{0:T(128)} %param.25) | copy-start | bytes 196
  0.0 13.9 %copy-start.8 = (f32[128]{0:T(128)S(1)}, f32[128]{0:T(128)}, u32[]{:S(2)}) copy-start(f32[128]{0:T(128)} %param.19) | copy-start | bytes 1540
  0.0 13.9 %copy-start.9 = (f32[128]{0:T(128)S(1)}, f32[128]{0:T(128)}, u32[]{:S(2)}) copy-start(f32[128]{0:T(128)} %param.18) | copy-start | bytes 1540
  1.6 22.0 %collective-permute-start.1 = (bf16[2,128,1536]{2,1,0:T(8,128)(2,1)S(1)}, bf16[2,128,1536]{2,1,0:T(8,128)(2,1)S(1)}, u32[]{:S(2)}, u32[]{:S(2)}) collective-permute-start(bf16[2,128,1536]{2,1,0:T(8,128)(2,1)S(1)} %get-tuple-element.21), channel_id=1, source_target_pairs={{0,1},{1,0},{2,3},{3,2},{4,5},{5,4},{6,7},{7,6},{8,9},{9,8},{10,11... | collective-permute-start | bytes 2359304 | tf_op jit(solution)/shard_map/ppermute | solution.py:449
  6.0 30.4 %all-to-all-start.2 = ((bf16[16,2,32,128]{3,2,1,0:T(8,128)(2,1)}), bf16[16,2,32,128]{3,2,1,0:T(8,128)(2,1)S(1)}, u32[]{:S(2)}, u32[]{:S(2)}) async-start(bf16[16,2,32,128]{3,2,1,0:T(8,128)(2,1)} %bitcast.10), calls=%async_computation.2 | async-start | bytes 524288 | tf_op jit(solution)/shard_map/all_to_all | solution.py:456
  23.6 0.9 copy-start.5
  36.3 57.7 %all-to-all-start.1 = ((bf16[16,3,128,128]{3,2,1,0:T(8,128)(2,1)}), bf16[16,3,128,128]{3,2,1,0:T(8,128)(2,1)S(1)}, u32[]{:S(2)}, u32[]{:S(2)}) async-start(bf16[16,3,128,128]{3,2,1,0:T(8,128)(2,1)} %bitcast.38), calls=%async_computation.1 | async-start | bytes 3145728 | tf_op jit(solution)/shard_map/all_to_all | solution.py:497
  42.0 39.2 %collective-permute-start = (bf16[2,128,1536]{2,1,0:T(8,128)(2,1)S(1)}, bf16[2,128,1536]{2,1,0:T(8,128)(2,1)S(1)}, u32[]{:S(2)}, u32[]{:S(2)}) collective-permute-start(bf16[2,128,1536]{2,1,0:T(8,128)(2,1)S(1)} %get-tuple-element.22), channel_id=1, source_target_pairs={{0,1},{1,0},{2,3},{3,2},{4,5},{5,4},{6,7},{7,6},{8,9},{9,8},{10,11... | collective-permute-start | bytes 2359304 | tf_op jit(solution)/shard_map/ppermute | solution.py:449
  46.4 53.8 %collective-permute-start.3 = (bf16[48,1536]{1,0:T(8,128)(2,1)}, bf16[48,1536]{1,0:T(8,128)(2,1)S(1)}, u32[]{:S(2)}, u32[]{:S(2)}) collective-permute-start(bf16[48,1536]{1,0:T(8,128)(2,1)} %dynamic_slice.6), channel_id=1, source_target_pairs={{0,1},{1,0},{2,3},{3,2},{4,5},{5,4},{6,7},{7,6},{8,9},{9,8},{10,11... | collective-permute-start | bytes 442376 | tf_op jit(solution)/shard_map/ppermute | solution.py:468
  81.3 0.9 copy-start.4
  94.1 12.2 %copy-start.3 = (bf16[16,3,128,128]{3,2,1,0:T(8,128)(2,1)}, bf16[16,3,128,128]{3,2,1,0:T(8,128)(2,1)S(1)}, u32[]{:S(2)}) copy-start(bf16[16,3,128,128]{3,2,1,0:T(8,128)(2,1)S(1)} %all-to-all-done.1.got_1) | copy-start | bytes 4718596
  94.1 32.4 %all-to-all-start = ((bf16[16,3,128,128]{3,2,1,0:T(8,128)(2,1)}), bf16[16,3,128,128]{3,2,1,0:T(8,128)(2,1)}, u32[]{:S(2)}, u32[]{:S(2)}) async-start(bf16[16,3,128,128]{3,2,1,0:T(8,128)(2,1)} %bitcast.39), calls=%async_computation | async-start | bytes 3145728 | tf_op jit(solution)/shard_map/all_to_all | solution.py:497
  100.2 23.1 %collective-permute-start.4 = (bf16[48,1536]{1,0:T(8,128)(2,1)S(1)}, bf16[48,1536]{1,0:T(8,128)(2,1)S(1)}, u32[]{:S(2)}, u32[]{:S(2)}) collective-permute-start(bf16[48,1536]{1,0:T(8,128)(2,1)S(1)} %collective-permute-done.3), channel_id=1, source_target_pairs={{0,8},{2,10},{4,12},{6,14},{8,16},{10,18},{12,20},{14,22},{16,24},... | collective-permute-start | bytes 442376 | tf_op jit(solution)/shard_map/ppermute | solution.py:505
  102.1 24.4 %collective-permute-start.5 = (bf16[48,1536]{1,0:T(8,128)(2,1)S(1)}, bf16[48,1536]{1,0:T(8,128)(2,1)S(1)}, u32[]{:S(2)}, u32[]{:S(2)}) collective-permute-start(bf16[48,1536]{1,0:T(8,128)(2,1)S(1)} %collective-permute-done.3), channel_id=1, source_target_pairs={{0,16},{2,18},{4,20},{6,22},{8,24},{10,26},{12,28},{14,30},{16,0},... | collective-permute-start | bytes 442376 | tf_op jit(solution)/shard_map/ppermute | solution.py:505
  104.8 52.1 %collective-permute-start.6 = (bf16[48,1536]{1,0:T(8,128)(2,1)S(1)}, bf16[48,1536]{1,0:T(8,128)(2,1)S(1)}, u32[]{:S(2)}, u32[]{:S(2)}) collective-permute-start(bf16[48,1536]{1,0:T(8,128)(2,1)S(1)} %collective-permute-done.3), channel_id=1, source_target_pairs={{0,24},{2,26},{4,28},{6,30},{8,0},{10,2},{12,4},{14,6},{16,8},{18,... | collective-permute-start | bytes 442376 | tf_op jit(solution)/shard_map/ppermute | solution.py:505
  152.8 54.1 %all-to-all-start.3 = ((bf16[32,144,256]{2,1,0:T(8,128)(2,1)}), bf16[32,144,256]{2,1,0:T(8,128)(2,1)S(1)}, u32[]{:S(2)}, u32[]{:S(2)}) async-start(bf16[32,144,256]{2,1,0:T(8,128)(2,1)} %bitcast.40), calls=%async_computation.3 | async-start | bytes 4718592 | tf_op jit(solution)/shard_map/all_to_all | solution.py:520
  156.9 17.8 %collective-permute-start.7 = (bf16[4,48,1536]{2,1,0:T(8,128)(2,1)S(1)}, bf16[4,48,1536]{2,1,0:T(8,128)(2,1)S(1)}, u32[]{:S(2)}, u32[]{:S(2)}) collective-permute-start(bf16[4,48,1536]{2,1,0:T(8,128)(2,1)S(1)} %bitcast_dynamic-update-slice_fusion.4), channel_id=1, source_target_pairs={{0,32},{32,64},{64,96},{96,0},{1,33},{33,65},{65,97},{97,1},{2,34}... | collective-permute-start | bytes 1769480 | tf_op jit(solution)/shard_map/ppermute | solution.py:511
  160.3 14.5 %copy-start.2 = (bf16[2,6,144,256]{3,2,1,0:T(8,128)(2,1)S(1)}, bf16[2,6,144,256]{3,2,1,0:T(8,128)(2,1)}, u32[]{:S(2)}) copy-start(bf16[2,6,144,256]{3,2,1,0:T(8,128)(2,1)} %diag.1.near) | copy-start | bytes 2654212
  160.3 28.3 %collective-permute-start.8 = (bf16[4,48,1536]{2,1,0:T(8,128)(2,1)S(1)}, bf16[4,48,1536]{2,1,0:T(8,128)(2,1)S(1)}, u32[]{:S(2)}, u32[]{:S(2)}) collective-permute-start(bf16[4,48,1536]{2,1,0:T(8,128)(2,1)S(1)} %bitcast_dynamic-update-slice_fusion.4), channel_id=1, source_target_pairs={{0,64},{32,96},{64,0},{96,32},{1,65},{33,97},{65,1},{97,33},{2,66}... | collective-permute-start | bytes 1769480 | tf_op jit(solution)/shard_map/ppermute | solution.py:511
  163.9 25.5 %collective-permute-start.9 = (bf16[4,48,1536]{2,1,0:T(8,128)(2,1)S(1)}, bf16[4,48,1536]{2,1,0:T(8,128)(2,1)S(1)}, u32[]{:S(2)}, u32[]{:S(2)}) collective-permute-start(bf16[4,48,1536]{2,1,0:T(8,128)(2,1)S(1)} %bitcast_dynamic-update-slice_fusion.4), channel_id=1, source_target_pairs={{0,96},{32,0},{64,32},{96,64},{1,97},{33,1},{65,33},{97,65},{2,98}... | collective-permute-start | bytes 1769480 | tf_op jit(solution)/shard_map/ppermute | solution.py:511
  174.8 32.1 %collective-permute-start.2 = (bf16[2,6,144,256]{3,2,1,0:T(8,128)(2,1)S(1)}, bf16[2,6,144,256]{3,2,1,0:T(8,128)(2,1)}, u32[]{:S(2)}, u32[]{:S(2)}) collective-permute-start(bf16[2,6,144,256]{3,2,1,0:T(8,128)(2,1)S(1)} %copy-done.2), channel_id=1, source_target_pairs={{0,1},{1,0},{2,3},{3,2},{4,5},{5,4},{6,7},{7,6},{8,9},{9,8},{10,11... | collective-permute-start | bytes 2654216 | tf_op jit(solution)/shard_map/ppermute | solution.py:516
  189.4 1.4 copy-start.1
  207.0 1.4 copy-start
